TPU v7x, 256 devices: a whole 4x4x8 slice. The times are simulated.
256 devices in a mesh: px: 16 (over z, y_hi), py: 16 (over x, y_lo, core).
Axes of the slice: x: 4, y: 4 (y_hi: 2, y_lo: 2; y = y_hi * 2 + y_lo), z: 8, core: 2. Of those that a mesh axis runs over, the one named last changes fastest.
Arguments:
- flow_field: bfloat16 [64, 128, 128, 128], P(None, 'px', 'py'), may hold values from -6 to 6
- cotangent: bfloat16 [64, 128, 128, 128], P(None, 'px', 'py'), may hold values from -6 to 6
- tucker_core: float32 [16, 16, 8, 8, 8], replicated, may hold values from -6 to 6
- in_factor: float32 [64, 16], replicated, may hold values from -0.75 to 0.75
- out_factor: float32 [64, 16], replicated, may hold values from -1.5 to 1.5
- first_factor: float32 [32, 8], replicated, may hold values from -2 to 2
- second_factor: float32 [32, 8], replicated, may hold values from -2 to 2
- third_factor: float32 [32, 8], replicated, may hold values from -2 to 2
Outputs:
- output_field: bfloat16 [64, 128, 128, 128], P(None, 'px', 'py')
- core_grad: float32 [16, 16, 8, 8, 8], replicated
- in_grad: float32 [64, 16], replicated
- out_grad: float32 [64, 16], replicated
- first_grad: float32 [32, 8], replicated
- second_grad: float32 [32, 8], replicated
- third_grad: float32 [32, 8], replicated
All inputs are finite; a program needn't handle non-finite values.
Results may differ from a plain program's by a relative error of at most 0.001.
Values sent between devices are 32-bit elements; how exact they have to be, the bound alone decides.
No kernel may reach another device: no remote copies, remote signals or barrier semaphores. Data moves between devices by JAX's collectives and lax.ppermute only.
A program may use at most 128 MiB of HBM per device.

v0:
```python
import math

import jax
import jax.numpy as jnp
from jax import lax
from jax.sharding import PartitionSpec as P

NX = 128
NY = 128
NZ = 128
M1 = 32
M2 = 32
M3 = 32


HIGHEST = lax.Precision.HIGHEST


def turn_table(count, length):
    position = jnp.arange(count)
    frequency = jnp.where(position < count // 2, position, position - count)
    cells_at = jnp.arange(length)
    phase = frequency[None, :] * cells_at[:, None] % length
    angle = 2.0 * math.pi / length * phase.astype(jnp.float32)
    cosine = jnp.cos(angle)
    sine = jnp.sin(angle)
    upper = jnp.stack([cosine, -sine], axis=1)
    lower = jnp.stack([sine, cosine], axis=1)
    return jnp.stack([upper, lower])


def depth_table(length, count):
    cells_at = jnp.arange(length)
    frequency = jnp.arange(count)
    phase = cells_at[:, None] * frequency[None, :] % length
    angle = 2.0 * math.pi / length * phase.astype(jnp.float32)
    return jnp.concatenate([jnp.cos(angle), -jnp.sin(angle)], axis=1)


def to_modes(fields, depth_tables):
    across = turn_table(M2, NY)
    along = turn_table(M1, NX)
    spectra = []
    for member, z_table in zip(fields, depth_tables):
        channels, rows_here, cols_here, depth_len = member.shape
        flat = jnp.dot(
            member.reshape(-1, depth_len).astype(jnp.float32), z_table, precision=HIGHEST
        )
        spectra.append(flat.reshape(channels, rows_here, cols_here, 2, M3))
    members = lax.all_to_all(tuple(spectra), "py", split_axis=4, concat_axis=2, tiled=True)
    lines = tuple(
        (jnp.einsum("cxypm,pyqk->cxqkm", member, across, precision=HIGHEST) for member in members)
    )
    members = (
        lax.all_to_all(lines[0], "px", split_axis=3, concat_axis=1, tiled=True),
        lax.all_to_all(lines[1], "px", split_axis=3, concat_axis=1, tiled=True),
    )
    return tuple(
        (jnp.einsum("cxpkm,pxqj->cqjkm", member, along, precision=HIGHEST) for member in members)
    )


def to_space(modes, depth_weights):
    across = turn_table(M2, NY)
    along = turn_table(M1, NX)
    depth_base = depth_table(NZ, M3).T.reshape(2, M3, NZ)
    lines = tuple(
        (jnp.einsum("cqjkm,pxqj->cpxkm", member, along, precision=HIGHEST) for member in modes)
    )
    members = (lax.all_to_all(lines[0], "px", split_axis=2, concat_axis=3, tiled=True),)
    columns = tuple(
        (jnp.einsum("cqxkm,pyqk->cpxym", member, across, precision=HIGHEST) for member in members)
    )
    members = (lax.all_to_all(columns[0], "py", split_axis=3, concat_axis=4, tiled=True),)
    return tuple(
        (
            jnp.einsum(
                "cpxyk,pkn->cxyn", member, depth_base * weight_row[None, :, None], precision=HIGHEST
            )
            for member, weight_row in zip(members, depth_weights)
        )
    )


def shards(
    flow_field,
    cotangent,
    tucker_core,
    in_factor,
    out_factor,
    first_factor,
    second_factor,
    third_factor,
):
    inverse_count = 1.0 / (NX * NY * NZ)
    weights = jnp.where(jnp.arange(M3) == 0, 1.0, 2.0).astype(jnp.float32)
    base_table = depth_table(NZ, M3)
    weighted_table = base_table * jnp.concatenate([weights, weights])[None, :]
    block_second = M2 // lax.axis_size("px")
    block_third = M3 // lax.axis_size("py")
    start_second = lax.axis_index("px") * block_second
    start_third = lax.axis_index("py") * block_third

    def build_kernel(core_arg, first_arg, second_arg, third_arg):
        second_rows = lax.dynamic_slice_in_dim(second_arg, start_second, block_second, 0)
        third_rows = lax.dynamic_slice_in_dim(third_arg, start_third, block_third, 0)
        partial_core = jnp.einsum("abrst,mt->abrsm", core_arg, third_rows, precision=HIGHEST)
        partial_core = jnp.einsum("abrsm,ks->abrkm", partial_core, second_rows, precision=HIGHEST)
        return jnp.einsum("abrkm,jr->abjkm", partial_core, first_arg, precision=HIGHEST)

    kernel, pullback = jax.vjp(build_kernel, tucker_core, first_factor, second_factor, third_factor)
    spectra, back = to_modes((flow_field, cotangent), (base_table, weighted_table))
    back = back * inverse_count
    lifted = jnp.einsum("ia,ipjkm->apjkm", in_factor, spectra, precision=HIGHEST)
    mixed = jnp.einsum("abjkm,apjkm->bpjkm", kernel, lifted, precision=HIGHEST)
    joined = jnp.einsum("ob,bpjkm->opjkm", out_factor, mixed, precision=HIGHEST)
    grids = to_space((joined,), (weights,))
    output_field = (grids[0] * inverse_count).astype(jnp.bfloat16)
    back_mixed = jnp.einsum("ob,opjkm->bpjkm", out_factor, back, precision=HIGHEST)
    grad_out = jnp.einsum("opjkm,bpjkm->ob", back, mixed, precision=HIGHEST)
    grad_kernel = jnp.einsum("bpjkm,apjkm->abjkm", back_mixed, lifted, precision=HIGHEST)
    back_lifted = jnp.einsum("abjkm,bpjkm->apjkm", kernel, back_mixed, precision=HIGHEST)
    grad_in = jnp.einsum("ipjkm,apjkm->ia", spectra, back_lifted, precision=HIGHEST)
    grad_core, grad_first, grad_second, grad_third = pullback(grad_kernel)
    totals = lax.psum(
        (grad_core, grad_in, grad_out, grad_first, grad_second, grad_third), ("px", "py")
    )
    return (output_field, totals[0], totals[1], totals[2], totals[3], totals[4], totals[5])


def solution(mesh):
    return jax.shard_map(
        shards,
        mesh=mesh,
        in_specs=(
            P(None, "px", "py", None),
            P(None, "px", "py", None),
            P(),
            P(),
            P(),
            P(),
            P(),
            P(),
        ),
        out_specs=(P(None, "px", "py", None), P(), P(), P(), P(), P(), P()),
        check_vma=False,
    )
```

profile of v0, /device:TPU:1, one launch (start us, length us, event | category | flops | bytes accessed | tf_op | source)
XLA Modules:
  0.0 434.1 jit_solution(5987552810933887608)
XLA Ops:
  8.4 2.2 convolution_bitcast_fusion
  10.6 1.8 copy.154
  12.4 3.7 reshape.164
  16.1 5.8 %copy.155 = f32[64,8,8,2,32]{0,2,3,1,4:T(8,128)S(1)} copy(f32[64,8,8,2,32]{4,3,2,1,0:T(2,128)} %reshape.164) | data formatting | bytes 2097152 | tf_op jit(solution)/shard_map/reshape | solution.py:49
  21.9 2.3 reshape.200
  24.2 7.4 %all-to-all-start.4 = ((f32[16,1,16384]{2,1,0:T(1,128)}), f32[16,1,16384]{2,1,0:T(1,128)}, u32[]{:S(2)}, u32[]{:S(2)}) async-start(f32[16,1,16384]{2,1,0:T(1,128)} %reshape.200), calls=%async_computation.4 | async-start | bytes 2097152 | tf_op jit(solution)/shard_map/all_to_all | solution.py:50
  33.4 3.7 reshape.161
  37.1 5.8 %copy.131 = f32[64,8,8,2,32]{0,2,3,1,4:T(8,128)S(1)} copy(f32[64,8,8,2,32]{4,3,2,1,0:T(2,128)} %reshape.161) | data formatting | bytes 2097152 | tf_op jit(solution)/shard_map/reshape | solution.py:49
  42.9 2.3 reshape.192
  45.2 2.1 all-to-all-done.4
  47.3 4.8 %all-to-all-start = ((f32[16,1,16384]{2,1,0:T(1,128)}), f32[16,1,16384]{2,1,0:T(1,128)S(1)}, u32[]{:S(2)}, u32[]{:S(2)}) async-start(f32[16,1,16384]{2,1,0:T(1,128)} %reshape.192), calls=%async_computation | async-start | bytes 2097152 | tf_op jit(solution)/shard_map/all_to_all | solution.py:50
  52.2 5.5 %convolution_bitcast_fusion.5 = f32[16,16,8,8,2]{1,4,3,2,0:T(2,128)S(1)} fusion(f32[16,16,8,8,8]{1,4,3,2,0:T(8,128)} %param.10, f32[32,8]{0,1:T(8,128)S(1)} %copy-done.18, s32[]{:T(128)S(6)} %select_n.81), kind=kOutput, calls=%fused_computation.14 | convolution fusion | flops 3145728 | bytes 656388 | tf_op jit(solution)/shard_map/jvp(abrst,mt->abrsm)/dot_general | solution.py:107
  58.2 4.3 reduce.4
  62.6 2.2 reshape.201
  64.7 3.0 fusion.10
  69.4 10.4 %all-to-all-start.5 = ((f32[16,1,4096]{2,1,0:T(1,128)}), f32[16,1,4096]{2,1,0:T(1,128)}, u32[]{:S(2)}, u32[]{:S(2)}) async-start(f32[16,1,4096]{2,1,0:T(1,128)} %reshape.202), calls=%async_computation.5 | async-start | bytes 524288 | tf_op jit(solution)/shard_map/all_to_all | solution.py:56
  80.9 1.8 convolution_bitcast_fusion.6
  82.7 3.1 reduce
  85.8 2.2 reshape.193
  88.0 3.0 fusion.7
  91.4 1.3 reshape.194
  92.7 9.8 %all-to-all-start.1 = ((f32[16,1,4096]{2,1,0:T(1,128)}), f32[16,1,4096]{2,1,0:T(1,128)}, u32[]{:S(2)}, u32[]{:S(2)}) async-start(f32[16,1,4096]{2,1,0:T(1,128)} %reshape.194), calls=%async_computation.1 | async-start | bytes 524288 | tf_op jit(solution)/shard_map/all_to_all | solution.py:55
  104.0 2.2 reduce.5
  108.4 6.1 %all-to-all-done.1 = f32[16,1,4096]{2,1,0:T(1,128)} async-done(((f32[16,1,4096]{2,1,0:T(1,128)}), f32[16,1,4096]{2,1,0:T(1,128)}, u32[]{:S(2)}, u32[]{:S(2)}) %all-to-all-start.1) | async-done | bytes 262176 | tf_op jit(solution)/shard_map/all_to_all | solution.py:55
  114.5 2.1 reduce.1
  118.9 2.8 convolution_bitcast_fusion.4
  121.7 1.8 copy.164
  124.3 3.7 convolution_bitcast_fusion.7
  129.9 2.6 convolution_bitcast_fusion.13
  135.0 1.9 copy.146
  136.9 2.3 reshape.196
  139.2 4.2 all-to-all-start.2
  143.6 5.2 %fusion.18 = f32[16,16,8,8,8]{1,4,3,2,0:T(8,128)} fusion(f32[16,16,8,8,2]{1,3,4,2,0:T(8,128)S(1)} %convolution_bitcast_fusion.3, f32[32,8]{0,1:T(8,128)S(1)} %copy-done.18, s32[]{:T(128)S(6)} %select_n.81), kind=kOutput, calls=%fused_computation.38 | convolution fusion | flops 3145728 | bytes 656388 | tf_op jit(solution)/shard_map/transpose(jvp(abrst,mt->abrsm))/dot_general | solution.py:107
  148.9 3.4 convolution_bitcast_fusion.20
  152.4 2.5 all-to-all-done.2
  154.9 2.1 reduce.2
  159.0 2.3 copy.150
  161.3 4.2 reshape.198
  165.4 8.2 %all-to-all-start.3 = ((f32[16,1,16384]{2,1,0:T(1,128)}), f32[16,1,16384]{2,1,0:T(1,128)}, u32[]{:S(2)}, u32[]{:S(2)}) async-start(f32[16,1,16384]{2,1,0:T(1,128)} %reshape.198), calls=%async_computation.3 | async-start | bytes 2097152 | tf_op jit(solution)/shard_map/all_to_all | solution.py:74
  173.6 10.9 %convolution_bitcast_fusion.19 = f32[2,8]{0,1:T(8,128)S(1)} fusion(f32[16,16,8,8,8]{1,4,3,2,0:T(8,128)} %param.10, f32[16,16,8,8,2]{1,3,4,2,0:T(8,128)S(1)} %convolution_bitcast_fusion.3), kind=kOutput, calls=%fused_computation.32 | convolution fusion | flops 3145728 | bytes 655424 | tf_op jit(solution)/shard_map/transpose(jvp(abrst,mt->abrsm))/dot_general | solution.py:107
  185.1 1.8 convolution_bitcast_fusion.12
  187.8 76.2 %all-reduce = (f32[64,16]{0,1:T(8,128)}, f32[64,16]{0,1:T(8,128)}, f32[32,8]{0,1:T(8,128)}, f32[32,8]{0,1:T(8,128)}, f32[32,8]{0,1:T(8,128)}) all-reduce(f32[64,16]{0,1:T(8,128)S(1)} %convolution_bitcast_fusion.18, f32[64,16]{0,1:T(8,128)S(1)} %convolution_bitcast_fusion.17, ...), channel_id=1, replica_groups=mesh['px'=16,'py'=16] {'px','py'}, use_global_device_ids=true, to_apply=%region_1.2 | all-reduce | flops 2816 | bytes 22528 | tf_op jit(solution)/shard_map/psum | solution.py:125
  264.0 4.3 reduce.3
  268.4 1.5 reshape.199
  271.3 4.7 %copy.153 = f32[64,2,8,8,32]{4,3,1,2,0:T(8,128)} copy(f32[64,2,8,8,32]{0,3,4,2,1:T(8,128)S(1)} %bitcast.258) | data formatting | bytes 2097152 | tf_op jit(solution)/shard_map/all_to_all | solution.py:74
  276.0 6.6 %fusion.5 = bf16[64,8,8,128]{3,2,1,0:T(8,128)(2,1)} fusion(f32[64,2,8,8,32]{4,3,1,2,0:T(8,128)} %copy.153, f32[2,32,128]{2,1,0:T(8,128)S(1)} %bitcast.273, f32[32]{0:T(128)S(1)} %compare_select_fusion.1), kind=kOutput, calls=%fused_computation.8 | convolution fusion | flops 403709952 | bytes 2130048 | tf_op jit(solution)/shard_map/cpxyk,pkn->cxyn/dot_general | solution.py:77
  282.6 139.5 %all-reduce.3.cloned.1.call-done = f32[16,16,8,8,8]{1,4,3,2,0:T(8,128)} async-done(((f32[16,16,8,8,8]{1,4,3,2,0:T(8,128)}), f32[16,16,8,8,8]{1,4,3,2,0:T(8,128)}) %all-reduce.3.cloned.1.call-update) | async-done | bytes 524304 | tf_op jit(solution)/shard_map/psum | solution.py:125
  422.1 4.9 %copy.281 = f32[16,16,8,8,8]{1,4,3,2,0:T(8,128)} copy(f32[16,16,8,8,8]{1,4,3,2,0:T(8,128)} %all-reduce.3.cloned.1.call-done) | data formatting | bytes 1048576
  (85 shorter events, 23.2 us)
Async XLA Ops:
  7.2 1.2 copy-start
  24.2 7.4 %copy-start.13 = (bf16[64,8,8,128]{3,2,1,0:T(8,128)(2,1)S(1)}, bf16[64,8,8,128]{3,2,1,0:T(8,128)(2,1)}, u32[]{:S(2)}) copy-start(bf16[64,8,8,128]{3,2,1,0:T(8,128)(2,1)} %param.8) | copy-start | bytes 3145732
  24.2 23.1 %all-to-all-start.4 = ((f32[16,1,16384]{2,1,0:T(1,128)}), f32[16,1,16384]{2,1,0:T(1,128)}, u32[]{:S(2)}, u32[]{:S(2)}) async-start(f32[16,1,16384]{2,1,0:T(1,128)} %reshape.200), calls=%async_computation.4 | async-start | bytes 2097152 | tf_op jit(solution)/shard_map/all_to_all | solution.py:50
  42.9 9.3 %copy-start.18 = (f32[32,8]{0,1:T(8,128)S(1)}, f32[32,8]{0,1:T(8,128)}, u32[]{:S(2)}) copy-start(f32[32,8]{0,1:T(8,128)} %param.15) | copy-start | bytes 3076
  47.3 22.1 %all-to-all-start = ((f32[16,1,16384]{2,1,0:T(1,128)}), f32[16,1,16384]{2,1,0:T(1,128)S(1)}, u32[]{:S(2)}, u32[]{:S(2)}) async-start(f32[16,1,16384]{2,1,0:T(1,128)} %reshape.192), calls=%async_computation | async-start | bytes 2097152 | tf_op jit(solution)/shard_map/all_to_all | solution.py:50
  64.7 15.0 %copy-start.17 = (f32[32,8]{0,1:T(8,128)S(1)}, f32[32,8]{0,1:T(8,128)}, u32[]{:S(2)}) copy-start(f32[32,8]{0,1:T(8,128)} %param.14) | copy-start | bytes 3076
  67.7 13.2 %copy-start.16 = (f32[32,8]{0,1:T(8,128)S(1)}, f32[32,8]{0,1:T(8,128)}, u32[]{:S(2)}) copy-start(f32[32,8]{0,1:T(8,128)} %param.13) | copy-start | bytes 3076
  69.4 23.3 %all-to-all-start.5 = ((f32[16,1,4096]{2,1,0:T(1,128)}), f32[16,1,4096]{2,1,0:T(1,128)}, u32[]{:S(2)}, u32[]{:S(2)}) async-start(f32[16,1,4096]{2,1,0:T(1,128)} %reshape.202), calls=%async_computation.5 | async-start | bytes 524288 | tf_op jit(solution)/shard_map/all_to_all | solution.py:56
  88.0 15.1 %copy-start.5 = (f32[16,16,32,2,2]{2,1,4,3,0:T(8,128)S(1)}, f32[16,16,32,2,2]{2,1,4,3,0:T(8,128)}, u32[]{:S(2)}) copy-start(f32[16,16,32,2,2]{2,1,4,3,0:T(8,128)} %convolution_bitcast_fusion.6) | copy-start | bytes 393220
  92.7 15.0 %copy-start.15 = (f32[64,16]{0,1:T(8,128)S(1)}, f32[64,16]{0,1:T(8,128)}, u32[]{:S(2)}) copy-start(f32[64,16]{0,1:T(8,128)} %param.12) | copy-start | bytes 12292
  92.7 21.8 %all-to-all-start.1 = ((f32[16,1,4096]{2,1,0:T(1,128)}), f32[16,1,4096]{2,1,0:T(1,128)}, u32[]{:S(2)}, u32[]{:S(2)}) async-start(f32[16,1,4096]{2,1,0:T(1,128)} %reshape.194), calls=%async_computation.1 | async-start | bytes 524288 | tf_op jit(solution)/shard_map/all_to_all | solution.py:55
  106.1 12.0 %copy-start.19 = (f32[64,16]{0,1:T(8,128)S(1)}, f32[64,16]{0,1:T(8,128)}, u32[]{:S(2)}) copy-start(f32[64,16]{0,1:T(8,128)} %param.11) | copy-start | bytes 12292
  107.0 0.7 copy-start.9
  108.4 15.1 %copy-start.6 = (f32[16,2,32,2,2]{0,1,4,3,2:T(2,128)}, f32[16,2,32,2,2]{0,1,4,3,2:T(2,128)S(1)}, u32[]{:S(2)}) copy-start(f32[16,2,32,2,2]{0,1,4,3,2:T(2,128)S(1)} %copy.163) | copy-start | bytes 49156
  117.5 0.6 copy-start.11
  118.9 4.6 %copy-start.8 = (f32[16,2,32,2,2]{0,1,4,3,2:T(2,128)}, f32[16,2,32,2,2]{0,1,4,3,2:T(2,128)S(1)}, u32[]{:S(2)}) copy-start(f32[16,2,32,2,2]{0,1,4,3,2:T(2,128)S(1)} %copy.142) | copy-start | bytes 49156
  123.5 0.8 copy-start.2
  128.1 0.7 copy-start.4
  139.2 15.6 %all-to-all-start.2 = ((f32[16,1,4096]{2,1,0:T(1,128)}), f32[16,1,4096]{2,1,0:T(1,128)}, u32[]{:S(2)}, u32[]{:S(2)}) async-start(f32[16,1,4096]{2,1,0:T(1,128)} %reshape.196), calls=%async_computation.2 | async-start | bytes 524288 | tf_op jit(solution)/shard_map/all_to_all | solution.py:70
  143.4 278.7 %all-reduce.3.cloned.1.call-start = ((), (), s32[]{:S(2)}) async-start(), calls=%async_computation.6 | async-start | bytes 8388608 | tf_op jit(solution)/shard_map/psum | solution.py:125
  165.4 98.6 %all-to-all-start.3 = ((f32[16,1,16384]{2,1,0:T(1,128)}), f32[16,1,16384]{2,1,0:T(1,128)}, u32[]{:S(2)}, u32[]{:S(2)}) async-start(f32[16,1,16384]{2,1,0:T(1,128)} %reshape.198), calls=%async_computation.3 | async-start | bytes 2097152 | tf_op jit(solution)/shard_map/all_to_all | solution.py:74
  173.6 11.2 %copy-start.10 = (f32[64,2,32,2,2]{0,2,4,3,1:T(8,128)S(1)}, f32[64,2,32,2,2]{0,2,4,3,1:T(8,128)}, u32[]{:S(2)}) copy-start(f32[64,2,32,2,2]{0,2,4,3,1:T(8,128)} %copy-done.9) | copy-start | bytes 196612
  173.6 11.5 %copy-start.7 = (f32[16,2,32,2,2]{0,1,4,3,2:T(2,128)S(1)}, f32[16,2,32,2,2]{0,1,4,3,2:T(2,128)}, u32[]{:S(2)}) copy-start(f32[16,2,32,2,2]{0,1,4,3,2:T(2,128)} %copy-done.6) | copy-start | bytes 49156
  173.6 13.3 %copy-start.12 = (f32[64,2,32,2,2]{0,2,4,3,1:T(8,128)S(1)}, f32[64,2,32,2,2]{0,2,4,3,1:T(8,128)}, u32[]{:S(2)}) copy-start(f32[64,2,32,2,2]{0,2,4,3,1:T(8,128)} %copy-done.11) | copy-start | bytes 196612
  184.6 2.7 copy-start.3
  271.3 4.7 %copy-start.14 = (f32[128,64]{0,1:T(8,128)S(1)}, f32[128,64]{0,1:T(8,128)}, u32[]{:S(2)}) copy-start(f32[128,64]{0,1:T(8,128)} %pad_maximum_fusion.1) | copy-start | bytes 98308
  422.1 4.9 %copy-start.1 = (bf16[64,8,8,128]{3,2,1,0:T(8,128)(2,1)S(1)}, bf16[64,8,8,128]{3,2,1,0:T(8,128)(2,1)}, u32[]{:S(2)}) copy-start(bf16[64,8,8,128]{3,2,1,0:T(8,128)(2,1)} %param.9) | copy-start | bytes 3145732
Sparse Core Ops, SparseCore 0:
  149.7 272.3 all-reduce.2
where the time goes:
time: 442 us; the launch traced here: 434 us
  waiting for transfers between devices  150 us (34%)
  blocking collectives  76.2 us (17%)
  local copies, waits for them, and re-layouts  67.3 us (15%)
  matrix products  61.7 us (14%)
  starting transfers between devices  44.8 us (10%)
  other arithmetic  19.1 us (4%)
  between operations  14.7 us (3%)
    psum x1, waiting for transfers between devices, shards(): lax.psum((grad_core, grad_in, grad_out, grad_first, grad_second, grad_thi...  140 us
    psum x1, blocking collectives, shards(): lax.psum((grad_core, grad_in, grad_out, grad_first, grad_second, grad_thi...  76.2 us
    unnamed x53, local copies, waits for them, and re-layouts  29.4 us
    dot_general x3, matrix products, build_kernel(): jnp.einsum('abrst,mt->abrsm', core_arg, third_rows, precision=HIGHEST)  21.7 us
    reshape x4, local copies, waits for them, and re-layouts, to_modes(): spectra.append(flat.reshape(channels, rows_here, cols_here, 2, M3))  18.9 us
    all_to_all x2, starting transfers between devices, to_modes(): lax.all_to_all(tuple(spectra), 'py', split_axis=4, concat_axis=2, tiled=T...  12.2 us
    all_to_all x1, starting transfers between devices, to_modes(): lax.all_to_all(lines[1], 'px', split_axis=3, concat_axis=1, tiled=True)  10.4 us
    all_to_all x1, starting transfers between devices, to_modes(): lax.all_to_all(lines[0], 'px', split_axis=3, concat_axis=1, tiled=True)  9.75 us
  transfers between devices with their start and end apart: 7, of which 4 were waited for; matrix products, arithmetic and copies ran while one was open for 23% of the time, Pallas kernels for 0%

commit v1 on v0

v1 whole, which is shorter than its diff:
```python
import functools

import jax
import jax.numpy as jnp
import numpy as np
from jax import lax
from jax.experimental import pallas as pl
from jax.experimental.pallas import tpu as pltpu
from jax.sharding import PartitionSpec as P

N = 128
F32 = jnp.float32
BF16 = jnp.bfloat16
NN = (((1,), (0,)), ((), ()))
NT = (((1,), (1,)), ((), ()))
TN = (((0,), (0,)), ((), ()))


def freq(k):
    return np.where(k < 16, k, k - 32)


def turn(phase, sign):
    angle = 2.0 * np.pi / N * np.mod(phase, N)
    c, s = np.cos(angle), sign * np.sin(angle)
    return np.stack([np.stack([c, s]), np.stack([-s, c])])


def split_table(table):
    hi = np.asarray(table, np.float32).astype(jnp.bfloat16)
    lo = (table - hi.astype(np.float64)).astype(np.float32).astype(jnp.bfloat16)
    return hi, lo


@functools.cache
def tables():
    i2, i8, i16 = np.arange(2), np.arange(8), np.arange(16)
    e2 = np.eye(2)
    z = np.arange(N)
    m = 2 * i16[:, None] + i2[None, :]
    ang = 2.0 * np.pi / N * np.mod(m[:, :, None] * z, N)
    tz = np.stack([np.cos(ang), -np.sin(ang)])
    zf = np.einsum("pdmz,yw->dypmwz", tz, e2).reshape(128, 256)
    zi = zf
    k = 2 * i16[:, None] + i2[None, :]
    y = 8 * i16[None, :, None] + 2 * np.arange(4)[:, None, None] + i2[None, None, :]
    ph = freq(k)[:, :, None, None, None] * y[None, None]
    tf = turn(ph, -1.0)
    yf = np.einsum("pqdkgsy,mn->dkmqgsypn", tf, e2).reshape(128, 512)
    ti = turn(ph, 1.0)
    yi = np.einsum("qpskgdy,mn->gdypmsknq", ti, e2).reshape(512, 128)
    x = 8 * i16[None, :] + i8[:, None]
    phx = x[:, :, None] * freq(np.arange(32))[None, None, :]
    tf = turn(phx, -1.0)
    e4 = np.eye(4).reshape(2, 2, 2, 2)
    xf = np.einsum("qrxsj,kmln->xskmqrlnj", tf, e4).reshape(1024, 256)
    ti = turn(phx, 1.0)
    xi = np.einsum("qrxdj,kmln->qkmjxdlnr", ti, e4).reshape(256, 1024)
    sel = np.zeros((8, 128, 2, 2, 4, 8), np.float32)
    for t in range(8):
        for bh in range(2):
            for mm in range(2):
                for r in range(8):
                    sel[t, bh * 16 + mm * 8 + r, r // 4, bh, r % 4, t] = 1.0
    sel = sel.reshape(1024, 128)
    sy = np.kron(np.eye(64), np.ones((8, 1)))
    out = {}
    for name, table in (("zf", zf), ("yf", yf), ("yi", yi), ("xf", xf), ("xi", xi), ("zi", zi)):
        hi, lo = split_table(table)
        axis = 1 if name in ("xf", "xi", "zi") else 0
        out[name] = np.concatenate([hi, lo], axis=axis) if name != "xf" and name != "xi" else np.stack([hi, lo])
    out["zi"] = np.stack(split_table(zi))
    out["sel"] = sel.astype(jnp.bfloat16)
    out["sy"] = sy.astype(np.float32).astype(jnp.bfloat16)
    return out


def split(v):
    hi = v.astype(BF16)
    return hi, (v - hi.astype(F32)).astype(BF16)


def split3(v):
    hi = v.astype(BF16)
    rest = v - hi.astype(F32)
    mid = rest.astype(BF16)
    return hi, mid, (rest - mid.astype(F32)).astype(BF16)


def mul(a, b, dims=NN):
    return lax.dot_general(a, b, dims, preferred_element_type=F32)


def rows_table(table, v, dims=NN):
    half = table.shape[0] // 2
    hi, lo = split(v)
    both = mul(table, hi, dims)
    return both[:half] + both[half:] + mul(table[:half], lo, dims)


def pick(v, table):
    hi, mid, lo = split3(v)
    return mul(hi, table) + mul(mid, table) + mul(lo, table)


def plane(ref, x):
    return ref[:, x].astype(F32).reshape(512, N).astype(BF16)


def fold_kernel(flow, cot, wk, zf, out, work):
    for f, field in enumerate((flow, cot)):
        w = wk[f]
        for pair in range(4):
            u = jnp.concatenate([plane(field, 2 * pair), plane(field, 2 * pair + 1)], axis=1)
            both = mul(w, u)
            v = both[:128] + both[128:]
            for x2 in range(2):
                row = ((2 * pair + x2) * 2 + f) * 16
                for yy in range(8):
                    work[yy // 2, row : row + 16, (yy % 2) * N : (yy % 2 + 1) * N] = v[
                        yy * 16 : yy * 16 + 16, x2 * N : (x2 + 1) * N
                    ]
    table = zf[...]
    for g in range(4):
        out[:, :, g * 256 : (g + 1) * 256] = rows_table(table, work[g], NT).reshape(16, 8, 256)


def y_kernel(data, yf, out):
    v = data[...].reshape(128, 1024)
    v = jnp.concatenate([v[:, g * 256 : (g + 1) * 256] for g in range(4)], axis=0)
    out[...] = rows_table(yf[...], v).reshape(16, 8, 256)


def prep_kernel(core, pack, kern, flat):
    for a in range(16):
        flat[a * 16 : (a + 1) * 16, :] = core[a].T
    f1, f2, f3 = pack[0:8], pack[8:16], pack[16:24]
    w = jnp.concatenate(
        [f1[r : r + 1] * f2[s : s + 1] * f3 for r in range(8) for s in range(8)], axis=0
    )
    wh, wl = split(w)
    ch, cl = split(flat[...])
    kern[...] = mul(ch, wh) + mul(cl, wh) + mul(ch, wl)


def mode_kernel(data, kern, pack, ex, xf, xi, out, gk):
    v = data[...].reshape(128, 256)
    t = jnp.concatenate([v[:, :128].T, v[:, 128:].T], axis=0)
    t = jnp.concatenate([t[x * 32 : (x + 1) * 32] for x in range(8)], axis=1)
    hi, lo = split(t)
    s = mul(hi, xf[0]) + mul(lo, xf[0]) + mul(hi, xf[1])
    wt = pack[24:25]
    lift = [s[:16, q * N : (q + 1) * N] for q in range(2)]
    back = [s[16:, q * N : (q + 1) * N] * wt for q in range(2)]
    mixed = [jnp.zeros((16, N), F32) for _ in range(2)]
    lows = [[], []]
    grads = []
    for a in range(16):
        k = kern[a * 16 : (a + 1) * 16]
        g = None
        for q in range(2):
            la = lift[q][a : a + 1]
            mixed[q] = mixed[q] + k * la
            lows[q].append(jnp.sum(k * back[q], axis=0, keepdims=True))
            g = back[q] * la if g is None else g + back[q] * la
        grads.append(g)
    low = [jnp.concatenate(rows, axis=0) for rows in lows]
    n = jnp.concatenate(
        [jnp.concatenate([mixed[q] * wt, low[q]], axis=0) for q in range(2)], axis=1
    )
    hi, lo = split(n)
    u = mul(hi, xi[0]) + mul(lo, xi[0]) + mul(hi, xi[1])
    u = jnp.concatenate([u[:, x * N : (x + 1) * N] for x in range(8)], axis=0)
    u = jnp.concatenate([u[:128].T, u[128:].T], axis=1)
    out[:, :, 0:256] = u.reshape(16, 8, 256)
    gall = jnp.concatenate(grads, axis=0)
    gk[...] = gall
    gh, gl = split(gall)
    eh, el = split(ex[...])
    gj = mul(gh, eh) + mul(gl, eh) + mul(gh, el)
    gj = gj.reshape(16, 2, 8, N)
    for a in range(16):
        out[a, :, 256:384] = gj[a, 0] + pltpu.roll(gj[a, 1], 64, 1)


def factor_kernel(gk, flat, pack, place, out):
    gh, gl = split(gk[...])
    ch, cl = split(flat[...])
    gw = mul(ch, gh, TN) + mul(cl, gh, TN) + mul(ch, gl, TN)
    f1, f2, f3 = pack[0:8], pack[8:16], pack[16:24]
    first, second = [None] * 8, [None] * 8
    third = None
    for r in range(8):
        for s in range(8):
            tile = gw[(r * 8 + s) * 8 : (r * 8 + s) * 8 + 8]
            t3 = tile * f3
            one = t3 * f2[s : s + 1]
            two = t3 * f1[r : r + 1]
            tri = tile * (f1[r : r + 1] * f2[s : s + 1])
            first[r] = one if first[r] is None else first[r] + one
            second[s] = two if second[s] is None else second[s] + two
            third = tri if third is None else third + tri
    one = jnp.concatenate([jnp.sum(v, axis=0, keepdims=True) for v in first], axis=0)
    two = jnp.concatenate([jnp.sum(v, axis=0, keepdims=True) for v in second], axis=0)
    out[...] = pick(one, place[0]) + pick(two, place[1]) + pick(third, place[2])


def unmode_kernel(data, yi, f2w, fact, out):
    table = yi[...]
    v = data[:, :, 0:256].reshape(128, 256)
    u = rows_table(table, v)
    for g in range(4):
        out[:, :, g * 256 : (g + 1) * 256] = u[g * 128 : (g + 1) * 128].reshape(16, 8, 256)
    lane = lax.broadcasted_iota(jnp.int32, (8, N), 1)
    extra = fact[...]
    for s in range(8):
        acc = jnp.zeros((8, N), F32)
        for d in range(16):
            acc = acc + data[d, :, 256:384] * f2w[d * 8 + s : d * 8 + s + 1]
        acc = acc + pltpu.roll(acc, N - 16, 1)
        acc = jnp.where(lane < 16, acc, pltpu.roll(acc, N - 48, 1))
        acc = jnp.where(lane < 32, acc, extra)
        out[2 * s, :, 1024:1152] = acc
        out[2 * s + 1, :, 1024:1152] = acc


def space_kernel(data, flow, cot, zi, f3w, sel, sy, out, vout, pacc):
    zh, zl = zi[0], zi[1]
    for g in range(4):
        v = data[:, :, g * 256 : (g + 1) * 256].reshape(128, 256)
        hi, lo = split(v)
        r = mul(hi, zh, TN) + mul(lo, zh, TN) + mul(hi, zl, TN)
        rh, rl = split(r)
        for x in range(8):
            for f in range(2):
                for y2 in range(2):
                    row = (2 * g + y2) * 16
                    src = slice(x * 32 + f * 16, x * 32 + f * 16 + 16)
                    lanes = slice(y2 * N, (y2 + 1) * N)
                    vout[f, row : row + 16, x * N : (x + 1) * N] = rh[src, lanes]
                    vout[f, 128 + row : 128 + row + 16, x * N : (x + 1) * N] = rl[src, lanes]
    ri = lax.broadcasted_iota(jnp.int32, (128, 512), 0) // 16
    ci = lax.broadcasted_iota(jnp.int32, (128, 512), 1) % 8
    same = ri == ci
    res = []
    for f, field in ((1, flow), (0, cot)):
        for pair in range(4):
            u = jnp.concatenate([plane(field, 2 * pair), plane(field, 2 * pair + 1)], axis=1)
            part = mul(vout[f, :, pair * 256 : (pair + 1) * 256], u, NT)
            if pair == 0:
                pacc[...] = part
            else:
                pacc[...] += part
        p = jnp.where(same, pacc[:128] + pacc[128:], 0.0)
        q = p[0:16]
        for yy in range(1, 8):
            q = q + p[yy * 16 : yy * 16 + 16]
        res.append(pick(q, sy[...]))
    both = jnp.concatenate(res, axis=1)
    fact = data[0, :, 1024:1152]
    for d in range(1, 16):
        fact = fact + data[d, :, 1024:1152]
    cols = []
    for t in range(8):
        acc = jnp.zeros((8, N), F32)
        for d in range(16):
            acc = acc + data[d, :, 1024:1152] * f3w[d * 8 + t : d * 8 + t + 1]
        cols.append(acc)
    core = pick(jnp.concatenate(cols, axis=1), sel[...])
    row = jnp.concatenate([both[0:8], both[8:16], fact, core], axis=1)
    for d in range(16):
        out[d] = row


def expand_kernel(vin, wk, out):
    w = wk[...]
    for pair in range(4):
        lanes = slice(pair * 256, (pair + 1) * 256)
        hi = vin[0, 0:128, lanes]
        lo = vin[0, 128:256, lanes]
        u = mul(w, jnp.concatenate([hi, lo, hi], axis=0))
        for x2 in range(2):
            out[:, 2 * pair + x2] = u[:, x2 * N : (x2 + 1) * N].reshape(64, 8, N).astype(BF16)


def gather_kernel(data, half, out, g1, g2, g3):
    total = data[0, :, 0:384]
    for d in range(1, 16):
        total = total + data[d, :, 0:384]
    fact = total[:, 256:384]
    g1[...] = pltpu.roll(fact, N - 32, 1)[:, :32]
    g2[...] = pltpu.roll(fact, N - 64, 1)[:, :32]
    g3[...] = pltpu.roll(fact, N - 96, 1)[:, :32]
    lane = lax.broadcasted_iota(jnp.int32, (8, N), 1)
    keep = half[...]
    mine = []
    for a in range(16):
        c = data[a, :, 384:512] * keep
        mine.append(c + pltpu.roll(c, 64, 1))
    tiles = []
    for bh in range(2):
        for q in range(4):
            tile = jnp.zeros((8, N), F32)
            for i in range(4):
                shift = (32 * i - 32 * bh) % N
                moved = mine[4 * q + i]
                moved = pltpu.roll(moved, shift, 1) if shift else moved
                tile = jnp.where(lane // 32 == i, moved, tile)
            tiles.append(tile)
    row = jnp.concatenate([total[:, 0:256]] + tiles, axis=1)
    for d in range(16):
        out[d] = row


def final_kernel(data, core, gin, gout):
    total = data[0, :, 0:256]
    for d in range(1, 16):
        total = total + data[d, :, 0:256]
    gin[0:8] = total[:, 0:64]
    gin[8:16] = total[:, 128:192]
    gout[0:8] = pltpu.roll(total[:, 0:128], 64, 1)[:, :64]
    gout[8:16] = pltpu.roll(total[:, 128:256], 64, 1)[:, :64]
    for d in range(16):
        s, rh = d // 2, d % 2
        c = jnp.concatenate([data[d, :, 256:768], data[d, :, 768:1280]], axis=0)
        core[:, rh * 4 : rh * 4 + 4, s] = c.T.reshape(16, 4, 8, 16)


def call(kernel, outs, scratch=(), flops=1_000_000):
    many = isinstance(outs, (list, tuple))
    shapes = [jax.ShapeDtypeStruct(*o) for o in outs] if many else jax.ShapeDtypeStruct(*outs.o)
    return pl.pallas_call(
        kernel,
        out_shape=shapes,
        scratch_shapes=list(scratch),
        cost_estimate=pl.CostEstimate(flops=flops, bytes_accessed=1_000_000, transcendentals=0),
        compiler_params=pltpu.CompilerParams(vmem_limit_bytes=48 * 1024 * 1024),
    )


def exchange(v, axis):
    return lax.all_to_all(v, axis, split_axis=0, concat_axis=0, tiled=True)


def halves(v):
    hi = lax.reduce_precision(v, 8, 7)
    return hi.astype(BF16), (v - hi).astype(BF16)


def shards(flow, cot, core, in_factor, out_factor, first, second, third):
    tab = {name: jnp.asarray(value) for name, value in tables().items()}
    px, py = lax.axis_index("px"), lax.axis_index("py")
    eye = jnp.eye(8, dtype=BF16)

    def fold(factor):
        parts = jnp.stack(halves(factor.T))
        return (eye[None, :, None, None, :] * parts[:, None, :, :, None]).reshape(256, 512)

    wk = jnp.stack([fold(in_factor), fold(out_factor)])
    oh, ol = halves(out_factor)
    parts = jnp.stack([oh, oh, ol])
    wk2 = (parts.transpose(1, 0, 2)[:, None, :, None, :] * eye[None, :, None, :, None]).reshape(512, 384)

    o1 = call(fold_kernel, [((16, 8, 1024), F32)], [pltpu.VMEM((4, 256, 256), F32)])(
        flow, cot, wk, tab["zf"]
    )[0]
    r1 = exchange(o1, "py")

    f1t, f2t, f3t = first.T, second.T, third.T
    f2own = lax.dynamic_slice_in_dim(f2t, 2 * px, 2, 1)
    f3own = lax.dynamic_slice_in_dim(f3t, 2 * py, 2, 1)
    shape = (8, 2, 2, 32)
    m = 2 * py + jnp.arange(2)
    weight = jnp.where(m == 0, 1.0, 2.0).astype(F32) * (1.0 / (N * N * N))
    pack = jnp.concatenate(
        [
            jnp.broadcast_to(f1t[:, None, None, :], shape),
            jnp.broadcast_to(f2own[:, :, None, None], shape),
            jnp.broadcast_to(f3own[:, None, :, None], shape),
            jnp.broadcast_to(weight[None, None, :, None], shape),
        ],
        axis=0,
    ).reshape(32, N)
    core_t = core.transpose(0, 2, 3, 4, 1).reshape(16, 512, 16)
    kern, flat = call(prep_kernel, [((256, N), F32), ((256, 512), F32)], flops=100_000_000)(core_t, pack)

    ex = jnp.pad(
        (jnp.eye(4, dtype=F32)[:, None, :, None] * first[None, :, None, :]).reshape(128, 32),
        ((0, 0), (0, 96)),
    )
    f2w = second.reshape(16, 2, 8).transpose(0, 2, 1)[:, :, None, None, :, None]
    f2w = jnp.broadcast_to(f2w, (16, 8, 2, 2, 2, 16)).reshape(128, N)
    f3w = third.reshape(16, 2, 8).transpose(0, 2, 1)[:, :, None, None, :, None]
    f3w = jnp.broadcast_to(f3w, (16, 8, 4, 2, 2, 8)).reshape(128, N)
    f3w = jnp.where(jnp.arange(N)[None, :] < 32, f3w, 0.0)
    lane_in = jnp.arange(N)[:, None]
    lane_out = jnp.arange(N)[None, :]
    place = jnp.stack(
        [
            lane_out == 32 + lane_in % 32,
            lane_out == 64 + 2 * px + lane_in // 64,
            lane_out == 96 + 2 * py + lane_in // 32 % 2,
        ]
    ).astype(BF16)
    half = jnp.broadcast_to((jnp.arange(N) // 64 == py % 2).astype(F32)[None, :], (8, N))

    o2 = call(y_kernel, [((16, 8, 256), F32)])(r1, tab["yf"])[0]
    r2 = exchange(o2, "px")
    o3, gk = call(mode_kernel, [((16, 8, 384), F32), ((256, N), F32)])(
        r2, kern, pack, ex, tab["xf"], tab["xi"]
    )
    r3 = exchange(o3, "px")
    fact = call(factor_kernel, [((8, N), F32)], flops=100_000_000)(gk, flat, pack, place)[0]
    o4 = call(unmode_kernel, [((16, 8, 1152), F32)])(r3, tab["yi"], f2w, fact)[0]
    r4 = exchange(o4, "py")
    o5, v = call(
        space_kernel,
        [((16, 8, 512), F32), ((2, 256, 1024), BF16)],
        [pltpu.VMEM((256, 512), F32)],
    )(r4, flow, cot, tab["zi"], f3w, tab["sel"], tab["sy"])
    r5 = exchange(o5, "px")
    field = call(expand_kernel, [((64, 8, 8, N), BF16)], flops=100_000_000)(v, wk2)[0]
    o6, g1, g2, g3 = call(
        gather_kernel, [((16, 8, 1280), F32), ((8, 32), F32), ((8, 32), F32), ((8, 32), F32)]
    )(r5, half)
    r6 = exchange(o6, "py")
    gcore, gin, gout = call(
        final_kernel, [((16, 8, 8, 8, 16), F32), ((16, 64), F32), ((16, 64), F32)]
    )(r6)
    return (field, gcore.transpose(0, 4, 1, 2, 3), gin.T, gout.T, g1.T, g2.T, g3.T)


def solution(mesh):
    spec = P(None, "px", "py", None)
    return jax.shard_map(
        shards,
        mesh=mesh,
        in_specs=(spec, spec, P(), P(), P(), P(), P(), P()),
        out_specs=(spec, P(), P(), P(), P(), P(), P()),
        check_vma=False,
    )
```

time: 442 us -> 133 us (0.30); the launches traced: 434 us -> 132 us
  waiting for transfers between devices: 150 us -> 36 us
  blocking collectives: 76.2 us -> 0 us
  matrix products: 61.7 us -> 0 us
  local copies, waits for them, and re-layouts: 67.3 us -> 27.9 us
  Pallas kernels: 0 us -> 15.8 us
  between operations: 14.7 us -> 1.03 us
  other arithmetic: 19.1 us -> 9.18 us
    psum x1 -> x0, waiting for transfers between devices: 140 us -> none  [shards(): lax.psum((grad_core, grad_in, grad_out, grad_first, grad_second, grad_thi...]
    psum x1 -> x0, blocking collectives: 76.2 us -> none  [shards(): lax.psum((grad_core, grad_in, grad_out, grad_first, grad_second, grad_thi...]
    dot_general x26 -> x0, matrix products: 61.7 us -> none  [the longest x3 21.7 us: build_kernel(): jnp.einsum('abrst,mt->abrsm', core_arg, third_rows, precision=HIGHEST)]
    all_to_all x6, waiting for transfers between devices: 10.6 us -> 36 us  [exchange(): return lax.all_to_all(v, axis, split_axis=0, concat_axis=0, tiled=True)]
    unnamed x53 -> x60, local copies, waits for them, and re-layouts: 29.4 us -> 10.7 us
    all_to_all x6 -> x0, other arithmetic: 18.2 us -> none  [the longest x2 7.39 us: to_modes(): lax.all_to_all(tuple(spectra), 'py', split_axis=4, concat_axis=2, tiled=T...]
    pallas_call x0 -> x10, Pallas kernels: none -> 15.8 us  [the longest x1 3.2 us: shards(): call(final_kernel, [((16, 8, 8, 8, 16), F32), ((16, 64), F32), ((16, 64),...]
    reshape x4, local copies, waits for them, and re-layouts: 18.9 us -> 3.53 us  [the longest x2 1.74 us: shards(): f3w = jnp.broadcast_to(f3w, (16, 8, 4, 2, 2, 8)).reshape(128, N)]
  transfers between devices with their start and end apart: 7 -> 6, of which waited for: 4 -> 6; matrix products, arithmetic and copies ran while one was open for 23% -> 14% of each run, Pallas kernels for 0% -> 3%
where the time goes in v1:
time: 133 us; the launch traced here: 132 us
  starting transfers between devices  42.4 us (32%)
  waiting for transfers between devices  36 us (27%)
  local copies, waits for them, and re-layouts  27.9 us (21%)
  Pallas kernels  15.8 us (12%)
  other arithmetic  9.18 us (7%)
    all_to_all x6, starting transfers between devices, exchange(): return lax.all_to_all(v, axis, split_axis=0, concat_axis=0, tiled=True)  42.4 us
    all_to_all x6, waiting for transfers between devices, exchange(): return lax.all_to_all(v, axis, split_axis=0, concat_axis=0, tiled=True)  36 us
    unnamed x60, local copies, waits for them, and re-layouts  10.7 us
    mul x4, local copies, waits for them, and re-layouts, fold(): eye[None, :, None, None, :] * parts[:, None, :, :, None]  5.64 us
    mul x1, local copies, waits for them, and re-layouts, shards(): parts.transpose(1, 0, 2)[:, None, :, None, :] * eye[None, :, None, :, None]  4.14 us
    pallas_call x1, Pallas kernels, shards(): call(final_kernel, [((16, 8, 8, 8, 16), F32), ((16, 64), F32), ((16, 64),...  3.2 us
  transfers between devices with their start and end apart: 6, of which 6 were waited for; matrix products, arithmetic and copies ran while one was open for 14% of the time, Pallas kernels for 3%

profile of v1, /device:TPU:1, one launch (start us, length us, event | category | flops | bytes accessed | tf_op | source)
XLA Modules:
  0.0 132.3 jit_solution(4814821429557030503)
XLA Ops:
  0.7 0.7 fusion.6
  1.4 0.7 fusion.7
  2.4 1.7 %broadcast_multiply_fusion.2 = (bf16[2,8,16,64,8]{2,1,0,4,3:T(8,128)(2,1)S(1)}, bf16[2,8,16,64,8]{2,1,0,4,3:T(8,128)(2,1)}) fusion(bf16[2,16,64]{1,0,2:T(2,128)(2,1)S(1)} %copy.28, bf16[8,8]{0,1:T(8,128)(2,1)S(1)} %copy.27, bf16[2,16,64]{1,0,2:T(2,128)(2,1)S(1)} %copy.29), kind=kLoop, calls=%fused_computation.2 | loop fusion | flops 262144 | bytes 532608 | tf_op jit(solution)/shard_map/mul | solution.py:357
  4.0 2.0 %mul.99 = bf16[1,256,512]{1,2,0:T(8,128)(2,1)S(1)} reshape(bf16[2,8,16,64,8]{2,1,0,4,3:T(8,128)(2,1)S(1)} %get-tuple-element.39) | data formatting | bytes 524288 | tf_op jit(solution)/shard_map/mul | solution.py:357
  6.2 3.4 %mul.102 = bf16[1,256,512]{1,2,0:T(8,128)(2,1)S(1)} reshape(bf16[2,8,16,64,8]{2,1,0,4,3:T(8,128)(2,1)} %get-tuple-element.40) | data formatting | bytes 524288 | tf_op jit(solution)/shard_map/mul | solution.py:357
  9.9 1.9 %shard_map.207 = f32[16,8,1024]{2,1,0:T(8,128)} custom-call(bf16[64,8,8,128]{3,2,1,0:T(8,128)(2,1)S(1)} %copy-done, bf16[64,8,8,128]{3,2,1,0:T(8,128)(2,1)S(1)} %copy-done.1, bf16[2,256,512]{2,1,0:T(8,128)(2,1)S(1)} %pad_maximum_fusion.wk, bf16[256,256]{1,0:T(8,128)(2,1)S(1)} %copy-done.16), custom_call_target="tpu_custom_call" | custom-call | flops 1000000 | bytes 1000000 | tf_op jit(solution)/shard_map/pallas_call | solution.py:364
  11.8 6.8 %all-to-all-start = ((f32[16,8,1024]{2,1,0:T(8,128)}), f32[16,8,1024]{2,1,0:T(8,128)S(1)}, u32[]{:S(2)}, u32[]{:S(2)}) async-start(f32[16,8,1024]{2,1,0:T(8,128)} %shard_map.207), calls=%async_computation | async-start | bytes 1048576 | tf_op jit(solution)/shard_map/all_to_all | solution.py:342
  19.7 8.6 %all-to-all-done.data = f32[16,8,1024]{2,1,0:T(8,128)S(1)} async-done(((f32[16,8,1024]{2,1,0:T(8,128)}), f32[16,8,1024]{2,1,0:T(8,128)S(1)}, u32[]{:S(2)}, u32[]{:S(2)}) %all-to-all-start) | async-done | bytes 524320 | tf_op jit(solution)/shard_map/all_to_all | solution.py:342
  28.3 0.9 shard_map.208
  29.3 10.6 %all-to-all-start.1 = ((f32[16,8,256]{2,1,0:T(8,128)}), f32[16,8,256]{2,1,0:T(8,128)S(1)}, u32[]{:S(2)}, u32[]{:S(2)}) async-start(f32[16,8,256]{2,1,0:T(8,128)} %shard_map.208), calls=%async_computation.1 | async-start | bytes 262144 | tf_op jit(solution)/shard_map/all_to_all | solution.py:342
  40.7 0.6 pad.4.ex
  41.4 2.2 %copy-done.2 = f32[16,16,8,8,8]{1,4,3,2,0:T(8,128)S(1)} copy-done((f32[16,16,8,8,8]{1,4,3,2,0:T(8,128)S(1)}, f32[16,16,8,8,8]{1,4,3,2,0:T(8,128)}, u32[]{:S(2)}) %copy-start.2) | copy-done | bytes 524312
  43.6 1.4 %shard_map.209 = (f32[256,128]{1,0:T(8,128)S(1)}, f32[256,512]{1,0:T(8,128)S(1)}) custom-call(f32[16,512,16]{2,1,0:T(8,128)S(1)} %bitcast.64, f32[32,128]{1,0:T(8,128)S(1)} %reshape.339.pack), custom_call_target="tpu_custom_call" | custom-call | flops 100000000 | bytes 1000000 | tf_op jit(solution)/shard_map/pallas_call | solution.py:385
  45.0 0.8 copy-done.7
  46.4 0.7 iota_compare_fusion.2
  47.1 2.8 %all-to-all-done.1.data = f32[16,8,256]{2,1,0:T(8,128)S(1)} async-done(((f32[16,8,256]{2,1,0:T(8,128)}), f32[16,8,256]{2,1,0:T(8,128)S(1)}, u32[]{:S(2)}, u32[]{:S(2)}) %all-to-all-start.1) | async-done | bytes 131104 | tf_op jit(solution)/shard_map/all_to_all | solution.py:342
  49.9 1.2 copy-done.4
  51.1 0.8 copy-done.12
  51.9 0.9 copy-done.18
  52.9 1.2 shard_map.210
  54.1 0.7 copy-done.13
  54.8 0.6 copy-done.19
  55.4 6.4 %all-to-all-start.2 = ((f32[16,8,384]{2,1,0:T(8,128)}), f32[16,8,384]{2,1,0:T(8,128)S(1)}, u32[]{:S(2)}, u32[]{:S(2)}) async-start(f32[16,8,384]{2,1,0:T(8,128)} %copy-done.13), calls=%async_computation.2 | async-start | bytes 393216 | tf_op jit(solution)/shard_map/all_to_all | solution.py:342
  61.8 0.7 iota_compare_fusion.1
  62.6 0.8 copy.33
  63.5 1.0 broadcast_in_dim.36
  64.5 1.7 %reshape.341.f2w = f32[128,128]{1,0:T(8,128)S(1)} reshape(f32[16,8,2,2,2,16]{5,4,3,2,1,0:T(2,128)} %broadcast_in_dim.36) | data formatting | bytes 131072 | tf_op jit(solution)/shard_map/reshape | solution.py:392
  66.2 0.7 iota_compare_fusion
  67.0 0.7 add_convert_fusion.place
  67.7 0.9 copy-done.20
  68.6 0.7 shard_map.211.fact
  69.3 3.1 %all-to-all-done.2.data = f32[16,8,384]{2,1,0:T(8,128)S(1)} async-done(((f32[16,8,384]{2,1,0:T(8,128)}), f32[16,8,384]{2,1,0:T(8,128)S(1)}, u32[]{:S(2)}, u32[]{:S(2)}) %all-to-all-start.2) | async-done | bytes 196640 | tf_op jit(solution)/shard_map/all_to_all | solution.py:342
  72.4 1.2 shard_map.212
  73.6 6.8 %all-to-all-start.3 = ((f32[16,8,1152]{2,1,0:T(8,128)}), f32[16,8,1152]{2,1,0:T(8,128)S(1)}, u32[]{:S(2)}, u32[]{:S(2)}) async-start(f32[16,8,1152]{2,1,0:T(8,128)} %shard_map.212), calls=%async_computation.3 | async-start | bytes 1179648 | tf_op jit(solution)/shard_map/all_to_all | solution.py:342
  80.5 1.1 broadcast_in_dim.38
  81.6 1.6 %reshape.343 = f32[128,128]{0,1:T(8,128)S(1)} reshape(f32[16,8,4,2,2,8]{1,0,5,4,3,2:T(8,128)} %broadcast_in_dim.38) | data formatting | bytes 131072 | tf_op jit(solution)/shard_map/reshape | solution.py:394
  83.4 7.3 %all-to-all-done.3.data = f32[16,8,1152]{2,1,0:T(8,128)S(1)} async-done(((f32[16,8,1152]{2,1,0:T(8,128)}), f32[16,8,1152]{2,1,0:T(8,128)S(1)}, u32[]{:S(2)}, u32[]{:S(2)}) %all-to-all-start.3) | async-done | bytes 589856 | tf_op jit(solution)/shard_map/all_to_all | solution.py:342
  90.7 2.5 %shard_map.213 = (f32[16,8,512]{2,1,0:T(8,128)}, bf16[2,256,1024]{2,1,0:T(8,128)(2,1)S(1)}) custom-call(f32[16,8,1152]{2,1,0:T(8,128)S(1)} %all-to-all-done.3.data, bf16[64,8,8,128]{3,2,1,0:T(8,128)(2,1)S(1)} %copy-done, bf16[64,8,8,128]{3,2,1,0:T(8,128)(2,1)S(1)} %copy-done.1, bf16[2,128,256]{2,1,0:T(8,128)(2,1)S(1)} %copy-done.15, ...), custom_call_target="tpu_custom_call" | custom-call | flops 1000000 | bytes 1000000 | tf_op jit(solution)/shard_map/pallas_call | solution.py:416
  93.3 1.0 copy-done.5
  94.2 5.0 %all-to-all-start.4 = ((f32[16,8,512]{2,1,0:T(8,128)}), f32[16,8,512]{2,1,0:T(8,128)S(1)}, u32[]{:S(2)}, u32[]{:S(2)}) async-start(f32[16,8,512]{2,1,0:T(8,128)} %get-tuple-element.25), calls=%async_computation.4 | async-start | bytes 524288 | tf_op jit(solution)/shard_map/all_to_all | solution.py:342
  99.3 11.3 %all-to-all-done.4.data = f32[16,8,512]{2,1,0:T(8,128)S(1)} async-done(((f32[16,8,512]{2,1,0:T(8,128)}), f32[16,8,512]{2,1,0:T(8,128)S(1)}, u32[]{:S(2)}, u32[]{:S(2)}) %all-to-all-start.4) | async-done | bytes 262176 | tf_op jit(solution)/shard_map/all_to_all | solution.py:342
  110.6 1.1 shard_map.215
  111.6 6.7 %all-to-all-start.5 = ((f32[16,8,1280]{2,1,0:T(8,128)}), f32[16,8,1280]{2,1,0:T(8,128)S(1)}, u32[]{:S(2)}, u32[]{:S(2)}) async-start(f32[16,8,1280]{2,1,0:T(8,128)} %get-tuple-element.26), calls=%async_computation.5 | async-start | bytes 1310720 | tf_op jit(solution)/shard_map/all_to_all | solution.py:342
  118.5 1.9 %broadcast_multiply_fusion = bf16[64,8,3,8,16]{4,3,2,1,0:T(8,128)(2,1)} fusion(bf16[8,8]{1,0:T(8,128)(2,1)S(1)} %copy-done.23, bf16[64,3,16]{2,1,0:T(4,128)(2,1)S(1)} %copy.38), kind=kLoop, calls=%fused_computation | loop fusion | flops 196608 | bytes 399488 | tf_op jit(solution)/shard_map/mul | solution.py:362
  120.4 4.1 %mul.113.wk = bf16[512,384]{1,0:T(8,128)(2,1)S(1)} reshape(bf16[64,8,3,8,16]{4,3,2,1,0:T(8,128)(2,1)} %broadcast_multiply_fusion) | data formatting | bytes 786432 | tf_op jit(solution)/shard_map/mul | solution.py:362
  124.6 1.7 %shard_map.214 = bf16[64,8,8,128]{3,2,1,0:T(8,128)(2,1)} custom-call(bf16[2,256,1024]{2,1,0:T(8,128)(2,1)S(1)} %copy-done.6, bf16[512,384]{1,0:T(8,128)(2,1)S(1)} %mul.113.wk), custom_call_target="tpu_custom_call" | custom-call | flops 100000000 | bytes 1000000 | tf_op jit(solution)/shard_map/pallas_call | solution.py:422
  126.2 2.9 %all-to-all-done.5.data = f32[16,8,1280]{2,1,0:T(8,128)S(1)} async-done(((f32[16,8,1280]{2,1,0:T(8,128)}), f32[16,8,1280]{2,1,0:T(8,128)S(1)}, u32[]{:S(2)}, u32[]{:S(2)}) %all-to-all-start.5) | async-done | bytes 655392 | tf_op jit(solution)/shard_map/all_to_all | solution.py:342
  129.1 3.2 %shard_map.216 = (f32[16,8,8,8,16]{4,3,2,1,0:T(8,128)}, f32[16,64]{1,0:T(8,128)}, f32[16,64]{1,0:T(8,128)}) custom-call(f32[16,8,1280]{2,1,0:T(8,128)S(1)} %all-to-all-done.5.data), custom_call_target="tpu_custom_call" | custom-call | flops 1000000 | bytes 1000000 | tf_op jit(solution)/shard_map/pallas_call | solution.py:427
  (84 shorter events, 3.7 us)
Async XLA Ops:
  0.6 1.5 %copy-start.22 = (bf16[8,8]{1,0:T(8,128)(2,1)}, bf16[8,8]{1,0:T(8,128)(2,1)S(1)}, u32[]{:S(2)}) copy-start(bf16[8,8]{1,0:T(8,128)(2,1)S(1)} %fusion.9) | copy-start | bytes 388
  6.2 3.6 %copy-start = (bf16[64,8,8,128]{3,2,1,0:T(8,128)(2,1)S(1)}, bf16[64,8,8,128]{3,2,1,0:T(8,128)(2,1)}, u32[]{:S(2)}) copy-start(bf16[64,8,8,128]{3,2,1,0:T(8,128)(2,1)} %flow.3) | copy-start | bytes 3145732
  6.2 3.6 %copy-start.1 = (bf16[64,8,8,128]{3,2,1,0:T(8,128)(2,1)S(1)}, bf16[64,8,8,128]{3,2,1,0:T(8,128)(2,1)}, u32[]{:S(2)}) copy-start(bf16[64,8,8,128]{3,2,1,0:T(8,128)(2,1)} %cot.3) | copy-start | bytes 3145732
  6.2 3.6 %copy-start.16 = (bf16[256,256]{1,0:T(8,128)(2,1)S(1)}, bf16[256,256]{1,0:T(8,128)(2,1)}, u32[]{:S(2)}) copy-start(bf16[256,256]{1,0:T(8,128)(2,1)} %constant.110.clone.zf) | copy-start | bytes 393220
  9.8 9.3 %copy-start.25 = (f32[32,8]{0,1:T(8,128)S(1)}, f32[32,8]{0,1:T(8,128)}, u32[]{:S(2)}) copy-start(f32[32,8]{0,1:T(8,128)} %param.22) | copy-start | bytes 3076
  9.8 9.4 %copy-start.26 = (f32[32,8]{0,1:T(8,128)S(1)}, f32[32,8]{0,1:T(8,128)}, u32[]{:S(2)}) copy-start(f32[32,8]{0,1:T(8,128)} %param.23) | copy-start | bytes 3076
  9.9 9.7 %copy-start.24 = (f32[32,8]{0,1:T(8,128)S(1)}, f32[32,8]{0,1:T(8,128)}, u32[]{:S(2)}) copy-start(f32[32,8]{0,1:T(8,128)} %param.21) | copy-start | bytes 3076
  9.9 18.4 %copy-start.11 = (bf16[256,512]{1,0:T(8,128)(2,1)S(1)}, bf16[256,512]{1,0:T(8,128)(2,1)}, u32[]{:S(2)}) copy-start(bf16[256,512]{1,0:T(8,128)(2,1)} %constant.111.clone.yf) | copy-start | bytes 786436
  11.8 16.5 %all-to-all-start = ((f32[16,8,1024]{2,1,0:T(8,128)}), f32[16,8,1024]{2,1,0:T(8,128)S(1)}, u32[]{:S(2)}, u32[]{:S(2)}) async-start(f32[16,8,1024]{2,1,0:T(8,128)} %shard_map.207), calls=%async_computation | async-start | bytes 1048576 | tf_op jit(solution)/shard_map/all_to_all | solution.py:342
  29.3 20.6 %all-to-all-start.1 = ((f32[16,8,256]{2,1,0:T(8,128)}), f32[16,8,256]{2,1,0:T(8,128)S(1)}, u32[]{:S(2)}, u32[]{:S(2)}) async-start(f32[16,8,256]{2,1,0:T(8,128)} %shard_map.208), calls=%async_computation.1 | async-start | bytes 262144 | tf_op jit(solution)/shard_map/all_to_all | solution.py:342
  41.4 2.2 %copy-start.2 = (f32[16,16,8,8,8]{1,4,3,2,0:T(8,128)S(1)}, f32[16,16,8,8,8]{1,4,3,2,0:T(8,128)}, u32[]{:S(2)}) copy-start(f32[16,16,8,8,8]{1,4,3,2,0:T(8,128)} %param.18) | copy-start | bytes 1572868
  43.6 2.9 %copy-start.28 = (s32[128]{0:T(128)S(1)}, s32[128]{0:T(128)}, u32[]{:S(2)}) copy-start(s32[128]{0:T(128)} %get-tuple-element.41) | copy-start | bytes 1540
  43.6 6.3 %copy-start.3 = (bf16[2,256,1024]{2,1,0:T(8,128)(2,1)S(1)}, bf16[2,256,1024]{2,1,0:T(8,128)(2,1)}, u32[]{:S(2)}) copy-start(bf16[2,256,1024]{2,1,0:T(8,128)(2,1)} %constant.114.clone.xi) | copy-start | bytes 3145732
  45.0 0.8 copy-start.7
  45.8 0.6 copy-start.17
  49.9 1.2 copy-start.4
  51.1 0.8 copy-start.12
  51.9 0.9 copy-start.18
  52.9 19.5 %copy-start.10 = (bf16[1024,128]{1,0:T(8,128)(2,1)S(1)}, bf16[1024,128]{1,0:T(8,128)(2,1)}, u32[]{:S(2)}) copy-start(bf16[1024,128]{1,0:T(8,128)(2,1)} %constant.112.clone.yi) | copy-start | bytes 786436
  54.1 0.7 copy-start.13
  54.8 0.6 copy-start.19
  55.4 12.3 %copy-start.8 = (f32[256,512]{1,0:T(8,128)S(1)}, f32[256,512]{1,0:T(8,128)}, u32[]{:S(2)}) copy-start(f32[256,512]{1,0:T(8,128)} %copy-done.7) | copy-start | bytes 1572868
  55.4 17.0 %all-to-all-start.2 = ((f32[16,8,384]{2,1,0:T(8,128)}), f32[16,8,384]{2,1,0:T(8,128)S(1)}, u32[]{:S(2)}, u32[]{:S(2)}) async-start(f32[16,8,384]{2,1,0:T(8,128)} %copy-done.13), calls=%async_computation.2 | async-start | bytes 393216 | tf_op jit(solution)/shard_map/all_to_all | solution.py:342
  63.5 16.9 %copy-start.27 = (f32[32,8]{0,1:T(8,128)S(1)}, f32[32,8]{0,1:T(8,128)}, u32[]{:S(2)}) copy-start(f32[32,8]{0,1:T(8,128)} %param.23) | copy-start | bytes 3076
  67.7 0.9 copy-start.20
  73.6 17.1 %copy-start.9 = (bf16[1024,128]{1,0:T(8,128)(2,1)S(1)}, bf16[1024,128]{1,0:T(8,128)(2,1)}, u32[]{:S(2)}) copy-start(bf16[1024,128]{1,0:T(8,128)(2,1)} %constant.116.clone.sel) | copy-start | bytes 786436
  73.6 17.1 %copy-start.14 = (bf16[512,64]{1,0:T(8,128)(2,1)S(1)}, bf16[512,64]{1,0:T(8,128)(2,1)}, u32[]{:S(2)}) copy-start(bf16[512,64]{1,0:T(8,128)(2,1)} %constant.117.clone.sy) | copy-start | bytes 196612
  73.6 17.1 %copy-start.15 = (bf16[2,128,256]{2,1,0:T(8,128)(2,1)S(1)}, bf16[2,128,256]{2,1,0:T(8,128)(2,1)}, u32[]{:S(2)}) copy-start(bf16[2,128,256]{2,1,0:T(8,128)(2,1)} %constant.115.clone.zi) | copy-start | bytes 393220
  73.6 17.1 %all-to-all-start.3 = ((f32[16,8,1152]{2,1,0:T(8,128)}), f32[16,8,1152]{2,1,0:T(8,128)S(1)}, u32[]{:S(2)}, u32[]{:S(2)}) async-start(f32[16,8,1152]{2,1,0:T(8,128)} %shard_map.212), calls=%async_computation.3 | async-start | bytes 1179648 | tf_op jit(solution)/shard_map/all_to_all | solution.py:342
  83.4 34.9 %copy-start.21 = (f32[64,16]{0,1:T(8,128)S(1)}, f32[64,16]{0,1:T(8,128)}, u32[]{:S(2)}) copy-start(f32[64,16]{0,1:T(8,128)} %param.20) | copy-start | bytes 12292
  83.4 35.1 %copy-start.23 = (bf16[8,8]{1,0:T(8,128)(2,1)S(1)}, bf16[8,8]{1,0:T(8,128)(2,1)}, u32[]{:S(2)}) copy-start(bf16[8,8]{1,0:T(8,128)(2,1)} %copy-done.22) | copy-start | bytes 388
  93.3 1.0 copy-start.5
  94.2 16.3 %all-to-all-start.4 = ((f32[16,8,512]{2,1,0:T(8,128)}), f32[16,8,512]{2,1,0:T(8,128)S(1)}, u32[]{:S(2)}, u32[]{:S(2)}) async-start(f32[16,8,512]{2,1,0:T(8,128)} %get-tuple-element.25), calls=%async_computation.4 | async-start | bytes 524288 | tf_op jit(solution)/shard_map/all_to_all | solution.py:342
  111.6 17.5 %all-to-all-start.5 = ((f32[16,8,1280]{2,1,0:T(8,128)}), f32[16,8,1280]{2,1,0:T(8,128)S(1)}, u32[]{:S(2)}, u32[]{:S(2)}) async-start(f32[16,8,1280]{2,1,0:T(8,128)} %get-tuple-element.26), calls=%async_computation.5 | async-start | bytes 1310720 | tf_op jit(solution)/shard_map/all_to_all | solution.py:342
  120.4 4.2 %copy-start.6 = (bf16[2,256,1024]{2,1,0:T(8,128)(2,1)S(1)}, bf16[2,256,1024]{2,1,0:T(8,128)(2,1)}, u32[]{:S(2)}) copy-start(bf16[2,256,1024]{2,1,0:T(8,128)(2,1)} %copy-done.5) | copy-start | bytes 3145732

commit v2 on v1

v2 whole, which is shorter than its diff:
```python
import functools

import jax
import jax.numpy as jnp
import numpy as np
from jax import lax
from jax.experimental import pallas as pl
from jax.experimental.pallas import tpu as pltpu
from jax.sharding import PartitionSpec as P

N = 128
F32 = jnp.float32
BF16 = jnp.bfloat16
NN = (((1,), (0,)), ((), ()))
NT = (((1,), (1,)), ((), ()))
TN = (((0,), (0,)), ((), ()))


def freq(k):
    return np.where(k < 16, k, k - 32)


def turn(phase, sign):
    angle = 2.0 * np.pi / N * np.mod(phase, N)
    c, s = np.cos(angle), sign * np.sin(angle)
    return np.stack([np.stack([c, s]), np.stack([-s, c])])


def split_table(table):
    hi = np.asarray(table, np.float32).astype(jnp.bfloat16)
    lo = (table - hi.astype(np.float64)).astype(np.float32).astype(jnp.bfloat16)
    return hi, lo


@functools.cache
def tables():
    i2, i8, i16 = np.arange(2), np.arange(8), np.arange(16)
    e2 = np.eye(2)
    z = np.arange(N)
    m = 2 * i16[:, None] + i2[None, :]
    ang = 2.0 * np.pi / N * np.mod(m[:, :, None] * z, N)
    tz = np.stack([np.cos(ang), -np.sin(ang)])
    zf = np.einsum("pdmz,yw->dypmwz", tz, e2).reshape(128, 256)
    k = 2 * i16[:, None] + i2[None, :]
    y = 8 * i16[None, :, None] + 2 * np.arange(4)[:, None, None] + i2[None, None, :]
    ph = freq(k)[:, :, None, None, None] * y[None, None]
    tf = turn(ph, -1.0)
    yf = np.einsum("pqdkgsy,mn->dkmqgsypn", tf, e2).reshape(128, 512)
    x = 8 * i16[None, :] + i8[:, None]
    phx = x[:, :, None] * freq(np.arange(32))[None, None, :]
    tf = turn(phx, -1.0)
    e4 = np.eye(4).reshape(2, 2, 2, 2)
    xf = np.einsum("qrxsj,kmln->xskmqrlnj", tf, e4).reshape(1024, 256)
    sel = np.zeros((8, 128, 2, 2, 4, 8), np.float32)
    for t in range(8):
        for bh in range(2):
            for mm in range(2):
                for r in range(8):
                    sel[t, bh * 16 + mm * 8 + r, r // 4, bh, r % 4, t] = 1.0
    sel = sel.reshape(1024, 128)
    sy = np.kron(np.eye(64), np.ones((8, 1)))
    return {
        "zf": np.concatenate(split_table(zf), axis=0),
        "yf": np.concatenate(split_table(yf), axis=0),
        "xf": np.stack(split_table(xf)),
        "sel": sel.astype(jnp.bfloat16),
        "sy": sy.astype(np.float32).astype(jnp.bfloat16),
    }


def split(v):
    hi = v.astype(BF16)
    return hi, (v - hi.astype(F32)).astype(BF16)


def split3(v):
    hi = v.astype(BF16)
    rest = v - hi.astype(F32)
    mid = rest.astype(BF16)
    return hi, mid, (rest - mid.astype(F32)).astype(BF16)


def mul(a, b, dims=NN):
    return lax.dot_general(a, b, dims, preferred_element_type=F32)


def rows_table(table, v, dims=NN):
    half = table.shape[0] // 2
    hi, lo = split(v)
    both = mul(table, hi, dims)
    return both[:half] + both[half:] + mul(table[:half], lo, dims)


def pick(v, table):
    hi, mid, lo = split3(v)
    return mul(hi, table) + mul(mid, table) + mul(lo, table)


def plane(ref, x):
    return ref[:, x].astype(F32).reshape(512, N).astype(BF16)


def spread(factor, sy):
    row = lax.broadcasted_iota(jnp.int32, (128, 512), 0) // 16
    col = lax.broadcasted_iota(jnp.int32, (128, 512), 1) % 8
    wide = [mul(part, sy, NT) for part in split(factor)]
    return [
        jnp.where(row == col, jnp.concatenate([w] * 8, axis=0), 0.0).astype(BF16) for w in wide
    ]


def fold_kernel(flow, cot, fin, fout, sy, zf, yf, out, yout, fields, tin, tout, tsy, tzf, work, sems):
    small = [
        pltpu.make_async_copy(src, dst, sems.at[8 + i])
        for i, (src, dst) in enumerate(((fin, tin), (fout, tout), (sy, tsy), (zf, tzf)))
    ]
    for copy in small:
        copy.start()
    get_yf = pltpu.make_async_copy(yf, yout, sems.at[12])
    large = []
    for f, field in enumerate((flow, cot)):
        for part in range(4):
            rows = pl.ds(16 * part, 16)
            copy = pltpu.make_async_copy(
                field.at[rows], fields.at[f, rows], sems.at[4 * f + part]
            )
            copy.start()
            large.append(copy)
    get_yf.start()
    for copy in small:
        copy.wait()
    for f, factor in enumerate((tin, tout)):
        w = jnp.concatenate(spread(factor[...], tsy[...]), axis=0)
        for copy in large[4 * f : 4 * f + 4]:
            copy.wait()
        for pair in range(4):
            u = jnp.concatenate(
                [plane(fields.at[f], 2 * pair), plane(fields.at[f], 2 * pair + 1)], axis=1
            )
            both = mul(w, u)
            v = both[:128] + both[128:]
            for x2 in range(2):
                row = ((2 * pair + x2) * 2 + f) * 16
                for yy in range(8):
                    work[yy // 2, row : row + 16, (yy % 2) * N : (yy % 2 + 1) * N] = v[
                        yy * 16 : yy * 16 + 16, x2 * N : (x2 + 1) * N
                    ]
    table = tzf[...]
    for g in range(4):
        out[:, :, g * 256 : (g + 1) * 256] = rows_table(table, work[g], NT).reshape(16, 8, 256)
    get_yf.wait()


def y_kernel(data, yf, out):
    v = data[...].reshape(128, 1024)
    v = jnp.concatenate([v[:, g * 256 : (g + 1) * 256] for g in range(4)], axis=0)
    out[...] = rows_table(yf[...], v).reshape(16, 8, 256)


def lanes(shape):
    return lax.broadcasted_iota(jnp.int32, shape, 0), lax.broadcasted_iota(jnp.int32, shape, 1)


def marks(cond):
    return jnp.where(cond, 1.0, 0.0).astype(BF16)


def prep_kernel(core, f1t, f2t, f3t, xf, kern, flat, xbuf, pack, ex, f2w, f3w, sem):
    get = pltpu.make_async_copy(xf, xbuf, sem)
    get.start()
    px, py = lax.axis_index("px"), lax.axis_index("py")
    row, lane = lanes((32, N))
    f1 = pick(f1t[...], marks(row == lane % 32))
    f2 = pick(f2t[...], marks(row == 2 * px + lane // 64))
    f3 = pick(f3t[...], marks(row == 2 * py + lane // 32 % 2))
    pack[0:8], pack[8:16], pack[16:24] = f1, f2, f3
    row, lane = lanes((8, N))
    pack[24:32] = jnp.where((py == 0) & (lane // 32 % 2 == 0), 1.0, 2.0) * (1.0 / (N * N * N))
    spread_r = marks(row == lane % 8)
    parts = split3(f1)
    wide = mul(parts[0], spread_r, TN) + mul(parts[1], spread_r, TN) + mul(parts[2], spread_r, TN)
    row, lane = lanes((N, N))
    ex[...] = jnp.where(row // 32 == lane // 8, wide, 0.0)
    for a in range(16):
        flat[a * 16 : (a + 1) * 16, :] = core[a].T
    w = jnp.concatenate(
        [f1[r : r + 1] * f2[s : s + 1] * f3 for r in range(8) for s in range(8)], axis=0
    )
    row, col = lanes((32, 16 * N))
    block, lane = col // N, col % N
    wide2 = pick(f2t[...], marks(row == 2 * block + lane // 16 % 2))
    wide3 = pick(f3t[...], marks((row == 2 * block + lane // 8 % 2) & (lane < 32)))
    for d in range(16):
        f2w[d * 8 : d * 8 + 8] = wide2[:, d * N : (d + 1) * N]
        f3w[d * 8 : d * 8 + 8] = wide3[:, d * N : (d + 1) * N]
    wh, wl = split(w)
    ch, cl = split(flat[...])
    kern[...] = mul(ch, wh) + mul(cl, wh) + mul(ch, wl)
    get.wait()


def mode_kernel(data, kern, pack, ex, xf, out, gk):
    v = data[...].reshape(128, 256)
    t = jnp.concatenate([v[:, :128].T, v[:, 128:].T], axis=0)
    t = jnp.concatenate([t[x * 32 : (x + 1) * 32] for x in range(8)], axis=1)
    hi, lo = split(t)
    s = mul(hi, xf[0]) + mul(lo, xf[0]) + mul(hi, xf[1])
    wt = pack[24:25]
    lift = [s[:16, q * N : (q + 1) * N] for q in range(2)]
    back = [s[16:, q * N : (q + 1) * N] * wt for q in range(2)]
    mixed = [jnp.zeros((16, N), F32) for _ in range(2)]
    lows = [[], []]
    grads = []
    for a in range(16):
        k = kern[a * 16 : (a + 1) * 16]
        g = None
        for q in range(2):
            la = lift[q][a : a + 1]
            mixed[q] = mixed[q] + k * la
            lows[q].append(jnp.sum(k * back[q], axis=0, keepdims=True))
            g = back[q] * la if g is None else g + back[q] * la
        grads.append(g)
    low = [jnp.concatenate(rows, axis=0) for rows in lows]
    gall = jnp.concatenate(grads, axis=0)
    gk[...] = gall
    n = jnp.concatenate(
        [jnp.concatenate([mixed[q] * wt, low[q]], axis=0) for q in range(2)], axis=1
    )
    hi, lo = split(n)
    u = mul(hi, xf[0], NT) + mul(lo, xf[0], NT) + mul(hi, xf[1], NT)
    u = jnp.concatenate([u[:, x * N : (x + 1) * N] for x in range(8)], axis=0)
    u = jnp.concatenate([u[:128].T, u[128:].T], axis=1)
    out[:, :, 0:256] = u.reshape(16, 8, 256)
    gh, gl = split(gall)
    eh, el = split(ex[...])
    gj = mul(gh, eh) + mul(gl, eh) + mul(gh, el)
    gj = gj.reshape(16, 2, 8, N)
    for a in range(16):
        out[a, :, 256:384] = gj[a, 0] + pltpu.roll(gj[a, 1], 64, 1)


def factor_grads(gk, flat, pack):
    gh, gl = split(gk[...])
    ch, cl = split(flat[...])
    gw = mul(ch, gh, TN) + mul(cl, gh, TN) + mul(ch, gl, TN)
    f1, f2, f3 = pack[0:8], pack[8:16], pack[16:24]
    first, second = [None] * 8, [None] * 8
    third = None
    for r in range(8):
        for s in range(8):
            tile = gw[(r * 8 + s) * 8 : (r * 8 + s) * 8 + 8]
            t3 = tile * f3
            one = t3 * f2[s : s + 1]
            two = t3 * f1[r : r + 1]
            tri = tile * (f1[r : r + 1] * f2[s : s + 1])
            first[r] = one if first[r] is None else first[r] + one
            second[s] = two if second[s] is None else second[s] + two
            third = tri if third is None else third + tri
    one = jnp.concatenate([jnp.sum(v, axis=0, keepdims=True) for v in first], axis=0)
    two = jnp.concatenate([jnp.sum(v, axis=0, keepdims=True) for v in second], axis=0)
    src, dst = lanes((N, N))
    total = jnp.zeros((8, N), F32)
    for v, lane in ((one, 96 + src % 32), (two, 64 + src // 64), (third, 66 + src // 32 % 2)):
        total = total + pick(v, marks(dst == lane))
    return total


def unmode_kernel(data, yf, f2w, gk, flat, pack, out, fact):
    hi, lo = split(data[:, :, 0:256].reshape(128, 256))
    u = mul(yf[...], jnp.concatenate([hi, hi], axis=0), TN) + mul(yf[:128], lo, TN)
    for g in range(4):
        out[:, :, g * 256 : (g + 1) * 256] = u[g * 128 : (g + 1) * 128].reshape(16, 8, 256)
    lane = lax.broadcasted_iota(jnp.int32, (8, N), 1)
    extra = factor_grads(gk, flat, pack)
    fact[...] = extra
    for s in range(8):
        acc = jnp.zeros((8, N), F32)
        for d in range(16):
            acc = acc + data[d, :, 256:384] * f2w[d * 8 + s : d * 8 + s + 1]
        acc = acc + pltpu.roll(acc, N - 16, 1)
        acc = jnp.where(lane < 16, acc, pltpu.roll(acc, N - 48, 1))
        acc = jnp.where(lane < 32, acc, extra)
        out[2 * s, :, 1024:1152] = acc
        out[2 * s + 1, :, 1024:1152] = acc


def space_kernel(
    data, zf, f3w, fact_in, sy, fout, flow, cot, sel, out, result, fields, vout, obuf, pacc, tsel, sems
):
    loads = []
    for f, field in enumerate((flow, cot)):
        for part in range(4):
            rows = pl.ds(16 * part, 16)
            load = pltpu.make_async_copy(
                field.at[rows], fields.at[f, rows], sems.at[4 * f + part]
            )
            load.start()
            loads.append(load)
    get_sel = pltpu.make_async_copy(sel, tsel, sems.at[8])
    get_sel.start()
    zh, zl = zf[:128], zf[128:]
    for g in range(4):
        v = data[:, :, g * 256 : (g + 1) * 256].reshape(128, 256)
        hi, lo = split(v)
        r = mul(hi, zh, TN) + mul(lo, zh, TN) + mul(hi, zl, TN)
        rh, rl = split(r)
        for x in range(8):
            for f in range(2):
                for y2 in range(2):
                    row = (2 * g + y2) * 16
                    src = slice(x * 32 + f * 16, x * 32 + f * 16 + 16)
                    cols = slice(y2 * N, (y2 + 1) * N)
                    vout[f, row : row + 16, x * N : (x + 1) * N] = rh[src, cols]
                    vout[f, 128 + row : 128 + row + 16, x * N : (x + 1) * N] = rl[src, cols]
    brow, bcol = lanes((16, N))
    repeat = marks(brow == bcol % 16)
    orow, ocol = lanes((512, N))
    wide = [
        jnp.where(orow % 8 == ocol // 16, mul(sy[...], mul(part, repeat, TN).astype(BF16)), 0.0)
        for part in split(fout[...])
    ]
    hi, lo = wide[0].astype(BF16), wide[1].astype(BF16)
    w = jnp.concatenate([hi, hi, lo], axis=1)
    for pair in range(4):
        cols = slice(pair * 256, (pair + 1) * 256)
        hi = vout[0, 0:128, cols]
        lo = vout[0, 128:256, cols]
        u = mul(w, jnp.concatenate([hi, lo, hi], axis=0))
        for x2 in range(2):
            obuf[:, 2 * pair + x2] = u[:, x2 * N : (x2 + 1) * N].reshape(64, 8, N).astype(BF16)
    puts = []
    for part in range(4):
        rows = pl.ds(16 * part, 16)
        put = pltpu.make_async_copy(obuf.at[rows], result.at[rows], sems.at[9 + part])
        put.start()
        puts.append(put)
    fact = data[0, :, 1024:1152]
    for d in range(1, 16):
        fact = fact + data[d, :, 1024:1152]
    cols = []
    for t in range(8):
        acc = jnp.zeros((8, N), F32)
        for d in range(16):
            acc = acc + data[d, :, 1024:1152] * f3w[d * 8 + t : d * 8 + t + 1]
        cols.append(acc)
    lane = lanes((8, N))[1]
    get_sel.wait()
    core = pick(jnp.concatenate(cols, axis=1), tsel[...])
    core = jnp.where(lane // 64 == lax.axis_index("py") % 2, core, 0.0)
    core = core + pltpu.roll(core, 64, 1)
    fact = jnp.where((lane == 66) | (lane == 67), fact_in[...], fact)
    last = jnp.where(lane < 64, core, fact)
    ri, ci = lanes((128, 512))
    same = ri // 16 == ci % 8
    res = []
    for f in range(2):
        field = fields.at[f]
        for load in loads[4 * f : 4 * f + 4]:
            load.wait()
        for pair in range(4):
            u = jnp.concatenate([plane(field, 2 * pair), plane(field, 2 * pair + 1)], axis=1)
            part = mul(vout[1 - f, :, pair * 256 : (pair + 1) * 256], u, NT)
            if pair == 0:
                pacc[...] = part
            else:
                pacc[...] += part
        p = jnp.where(same, pacc[:128] + pacc[128:], 0.0)
        q = p[0:16]
        for yy in range(1, 8):
            q = q + p[yy * 16 : yy * 16 + 16]
        res.append(pick(q, sy[...]))
    both = jnp.concatenate(res, axis=1)
    row = jnp.concatenate([both[0:8], both[8:16], last], axis=1)
    for d in range(16):
        out[d] = row
    for put in puts:
        put.wait()


def gather_kernel(data, out, g1, g2):
    total = data[0]
    for d in range(1, 16):
        total = total + data[d]
    fact = total[:, 256:384]
    g1[...] = pltpu.roll(fact, N - 96, 1)[:, :32]
    lane = lax.broadcasted_iota(jnp.int32, (8, N), 1)
    second = jnp.zeros((8, N), F32)
    for d in range(16):
        moved = pltpu.roll(data[d, :, 256:384], (2 * d - 64) % N, 1)
        second = jnp.where(lane // 2 == d, moved, second)
    g2[...] = second[:, :32]
    tiles = []
    for bh in range(2):
        for q in range(4):
            tile = jnp.zeros((8, N), F32)
            for i in range(4):
                shift = (32 * i - 32 * bh) % N
                moved = data[4 * q + i, :, 256:384]
                moved = pltpu.roll(moved, shift, 1) if shift else moved
                tile = jnp.where(lane // 32 == i, moved, tile)
            tiles.append(tile)
    row = jnp.concatenate([total[:, 0:256]] + tiles + [fact], axis=1)
    for d in range(16):
        out[d] = row


def final_kernel(data, core, gin, gout, g3, buf, sems):
    sends = []
    for q in range(4):
        for d in range(16):
            lo, hi = 256 + q * N, 768 + q * N
            c = jnp.concatenate([data[d, :, lo : lo + N], data[d, :, hi : hi + N]], axis=0)
            rows = slice(d % 2 * 4, d % 2 * 4 + 4)
            buf[4 * q : 4 * q + 4, rows, d // 2] = c.T.reshape(4, 4, 8, 16)
        part = pl.ds(4 * q, 4)
        send = pltpu.make_async_copy(buf.at[part], core.at[part], sems.at[q])
        send.start()
        sends.append(send)
    total = data[0, :, 0:256]
    for d in range(1, 16):
        total = total + data[d, :, 0:256]
    gin[0:8] = total[:, 0:64]
    gin[8:16] = total[:, 128:192]
    gout[0:8] = pltpu.roll(total[:, 0:128], 64, 1)[:, :64]
    gout[8:16] = pltpu.roll(total[:, 128:256], 64, 1)[:, :64]
    lane = lax.broadcasted_iota(jnp.int32, (8, N), 1)
    third = jnp.zeros((8, N), F32)
    for d in range(16):
        moved = pltpu.roll(data[d, :, 1280:1408], (2 * d - 66) % N, 1)
        third = jnp.where(lane // 2 == d, moved, third)
    g3[...] = third[:, :32]
    for send in sends:
        send.wait()


VM = pl.BlockSpec(memory_space=pltpu.VMEM)
HB = pl.BlockSpec(memory_space=pltpu.HBM)
DMA = pltpu.SemaphoreType.DMA


def call(kernel, ins, outs, scratch=(), flops=1_000_000, vmem=12):
    shapes = [
        pltpu.HBM(*o[:2]) if len(o) > 2 and o[2] is HB
        else jax.ShapeDtypeStruct(*o)
        for o in outs
    ]
    run = pl.pallas_call(
        kernel,
        out_shape=shapes,
        in_specs=[VM] * ins[0] + [HB] * ins[1],
        out_specs=[o[2] if len(o) > 2 else VM for o in outs],
        scratch_shapes=list(scratch),
        cost_estimate=pl.CostEstimate(flops=flops, bytes_accessed=1_000_000, transcendentals=0),
        compiler_params=pltpu.CompilerParams(vmem_limit_bytes=vmem * 1024 * 1024),
    )

    def placed(*args):
        far = [pltpu.with_memory_space_constraint(v, pltpu.HBM) for v in args[ins[0] :]]
        return run(*args[: ins[0]], *far)

    return placed


def exchange(v, axis):
    return lax.all_to_all(v, axis, split_axis=0, concat_axis=0, tiled=True)


def shards(flow, cot, core, in_factor, out_factor, first, second, third):
    tab = {name: jnp.asarray(value) for name, value in tables().items()}
    fin, fout = in_factor.T, out_factor.T

    o1, yf = call(
        fold_kernel,
        (0, 7),
        [((16, 8, 1024), F32), ((256, 512), BF16)],
        [
            pltpu.VMEM((2, 64, 8, 8, N), BF16),
            pltpu.VMEM((16, 64), F32),
            pltpu.VMEM((16, 64), F32),
            pltpu.VMEM((512, 64), BF16),
            pltpu.VMEM((256, 256), BF16),
            pltpu.VMEM((4, 256, 256), F32),
            DMA((13,)),
        ],
    )(flow, cot, fin, fout, tab["sy"], tab["zf"], tab["yf"])
    r1 = exchange(o1, "py")
    r1, core, first, second, third = lax.optimization_barrier((r1, core, first, second, third))
    f1t, f2t, f3t = first.T, second.T, third.T
    core_t = core.transpose(0, 2, 3, 4, 1).reshape(16, 512, 16)
    kern, flat, xf, pack, ex, f2w, f3w = call(
        prep_kernel,
        (4, 1),
        [
            ((256, N), F32),
            ((256, 512), F32),
            ((2, 1024, 256), BF16),
            ((32, N), F32),
            ((N, N), F32),
            ((N, N), F32),
            ((N, N), F32),
        ],
        [DMA],
        flops=100_000_000,
    )(core_t, f1t, f2t, f3t, tab["xf"])
    o2 = call(y_kernel, (2, 0), [((16, 8, 256), F32)])(r1, yf)[0]
    r2 = exchange(o2, "px")
    o3, gk = call(mode_kernel, (5, 0), [((16, 8, 384), F32), ((256, N), F32)])(
        r2, kern, pack, ex, xf
    )
    r3 = exchange(o3, "px")
    o4, fact = call(unmode_kernel, (6, 0), [((16, 8, 1152), F32), ((8, N), F32)])(
        r3, yf, f2w, gk, flat, pack
    )
    r4 = exchange(o4, "py")
    o5, field = call(
        space_kernel,
        (6, 3),
        [((16, 8, 384), F32), ((64, 8, 8, N), BF16, HB)],
        [
            pltpu.VMEM((2, 64, 8, 8, N), BF16),
            pltpu.VMEM((2, 256, 1024), BF16),
            pltpu.VMEM((64, 8, 8, N), BF16),
            pltpu.VMEM((256, 512), F32),
            pltpu.VMEM((1024, N), BF16),
            DMA((13,)),
        ],
    )(r4, tab["zf"], f3w, fact, tab["sy"], fout, flow, cot, tab["sel"])
    r5 = exchange(o5, "px")
    o6, g1, g2 = call(
        gather_kernel, (1, 0), [((16, 8, 1408), F32), ((8, 32), F32), ((8, 32), F32)]
    )(r5)
    r6 = exchange(o6, "py")
    gcore, gin, gout, g3 = call(
        final_kernel,
        (1, 0),
        [((16, 8, 8, 8, 16), F32, HB), ((16, 64), F32), ((16, 64), F32), ((8, 32), F32)],
        [pltpu.VMEM((16, 8, 8, 8, 16), F32), DMA((4,))],
    )(r6)
    return (field, gcore.transpose(0, 4, 1, 2, 3), gin.T, gout.T, g1.T, g2.T, g3.T)


def solution(mesh):
    spec = P(None, "px", "py", None)
    return jax.shard_map(
        shards,
        mesh=mesh,
        in_specs=(spec, spec, P(), P(), P(), P(), P(), P()),
        out_specs=(spec, P(), P(), P(), P(), P(), P()),
        check_vma=False,
    )
```

time: 133 us -> 113 us (0.85)
  blocking collectives: 0 us -> 78.2 us
  starting transfers between devices: 42.4 us -> 10.6 us
  waiting for transfers between devices: 36 us -> 6.16 us
  local copies, waits for them, and re-layouts: 27.9 us -> 2.21 us
  other arithmetic: 9.18 us -> 0 us
    all_to_all x0 -> x5, blocking collectives: none -> 78.2 us  [exchange(): return lax.all_to_all(v, axis, split_axis=0, concat_axis=0, tiled=True)]
    all_to_all x6 -> x1, starting transfers between devices: 42.4 us -> 10.6 us  [exchange(): return lax.all_to_all(v, axis, split_axis=0, concat_axis=0, tiled=True)]
    all_to_all x6 -> x1, waiting for transfers between devices: 36 us -> 6.16 us  [exchange(): return lax.all_to_all(v, axis, split_axis=0, concat_axis=0, tiled=True)]
    mul x7 -> x0, local copies, waits for them, and re-layouts: 9.97 us -> none  [the longest x4 5.64 us: fold(): eye[None, :, None, None, :] * parts[:, None, :, :, None]]
    unnamed x60 -> x14, local copies, waits for them, and re-layouts: 10.7 us -> 2.21 us
    mul x4 -> x0, other arithmetic: 3.69 us -> none  [the longest x1 1.94 us: shards(): parts.transpose(1, 0, 2)[:, None, :, None, :] * eye[None, :, None, :, None]]
    reshape x4 -> x0, local copies, waits for them, and re-layouts: 3.53 us -> none  [the longest x2 1.74 us: shards(): f3w = jnp.broadcast_to(f3w, (16, 8, 4, 2, 2, 8)).reshape(128, N)]
    broadcast_in_dim x7 -> x0, local copies, waits for them, and re-layouts: 2.31 us -> none  [the longest x1 1.07 us: shards(): f3w = jnp.broadcast_to(f3w, (16, 8, 4, 2, 2, 8)).reshape(128, N)]
  transfers between devices with their start and end apart: 6 -> 1, of which waited for: 6 -> 1; matrix products, arithmetic and copies ran while one was open for 14% -> 0% of each run, Pallas kernels for 3% -> 1%
where the time goes in v2:
time: 113 us
  blocking collectives  78.2 us (69%)
  Pallas kernels  14.8 us (13%)
  starting transfers between devices  10.6 us (9%)
  waiting for transfers between devices  6.16 us (5%)
  local copies, waits for them, and re-layouts  2.21 us (2%)
    all_to_all x5, blocking collectives, exchange(): return lax.all_to_all(v, axis, split_axis=0, concat_axis=0, tiled=True)  78.2 us
    pallas_call x8, Pallas kernels, placed(): return run(*args[:ins[0]], *far)  14.8 us
    all_to_all x1, starting transfers between devices, exchange(): return lax.all_to_all(v, axis, split_axis=0, concat_axis=0, tiled=True)  10.6 us
    all_to_all x1, waiting for transfers between devices, exchange(): return lax.all_to_all(v, axis, split_axis=0, concat_axis=0, tiled=True)  6.16 us
  transfers between devices with their start and end apart: 1, of which 1 were waited for; matrix products, arithmetic and copies ran while one was open for 0% of the time, Pallas kernels for 1%

profile of v2, /device:TPU:1, one launch (start us, length us, event | category | flops | bytes accessed | tf_op | source)
XLA Modules:
  0.0 112.7 jit_solution(5199608885310445937)
XLA Ops:
  0.6 0.0 copy-start.6
  0.6 0.0 copy-start.5
  0.7 0.0 copy-start.4
  0.7 2.8 %shard_map.180 = (f32[16,8,1024]{2,1,0:T(8,128)S(1)}, bf16[256,512]{1,0:T(8,128)(2,1)S(1)}) custom-call(bf16[64,8,8,128]{3,2,1,0:T(8,128)(2,1)} %flow.3, bf16[64,8,8,128]{3,2,1,0:T(8,128)(2,1)} %cot.3, f32[16,64]{1,0:T(8,128)} %bitcast.20, f32[16,64]{1,0:T(8,128)} %bitcast.15, bf16[512,64]{1,0:T(8,128)(2,1)} %constant.14.clone.sy, ...), custom_call_target="tpu_custom_call" | custom-call | flops 1000000 | bytes 1000000 | tf_op jit(solution)/shard_map/pallas_call | solution.py:459
  3.5 16.3 %all_to_all.30.data = f32[16,8,1024]{2,1,0:T(8,128)S(1)} all-to-all(f32[16,8,1024]{2,1,0:T(8,128)S(1)} %get-tuple-element.34), channel_id=1, replica_groups=mesh['px'=16,'py'=16] {'py'}, dimensions={0} | all-to-all | bytes 1048576 | tf_op jit(solution)/shard_map/all_to_all | solution.py:465
  19.8 0.9 shard_map.181
  20.8 10.6 %all-to-all-start.1 = ((f32[16,8,256]{2,1,0:T(8,128)}), f32[16,8,256]{2,1,0:T(8,128)S(1)}, u32[]{:S(2)}, u32[]{:S(2)}) async-start(f32[16,8,256]{2,1,0:T(8,128)} %shard_map.181), calls=%async_computation.1 | async-start | bytes 262144 | tf_op jit(solution)/shard_map/all_to_all | solution.py:465
  31.4 0.0 copy-done.6
  31.4 0.0 copy-done.5
  31.4 0.0 copy-done.4
  31.4 0.0 copy-start
  31.4 2.2 %copy-done = f32[16,16,8,8,8]{1,4,3,2,0:T(8,128)S(1)} copy-done((f32[16,16,8,8,8]{1,4,3,2,0:T(8,128)S(1)}, f32[16,16,8,8,8]{1,4,3,2,0:T(8,128)}, u32[]{:S(2)}) %copy-start) | copy-done | bytes 524312
  33.6 0.0 copy-start.1
  33.6 0.0 copy-start.2
  33.6 0.0 copy-start.3
  33.6 1.6 %shard_map.182 = (f32[256,128]{1,0:T(8,128)S(1)}, f32[256,512]{1,0:T(8,128)S(1)}, bf16[2,1024,256]{2,1,0:T(8,128)(2,1)S(1)}, f32[32,128]{1,0:T(8,128)S(1)}, f32[...) custom-call(f32[16,512,16]{2,1,0:T(8,128)S(1)} %bitcast.14, f32[8,32]{1,0:T(8,128)S(1)} %bitcast.17, ...), custom_call_target="tpu_custom_call" | custom-call | flops 100000000 | bytes 1000000 | tf_op jit(solution)/shard_map/pallas_call | solution.py:459
  35.2 6.2 %all-to-all-done.1.data = f32[16,8,256]{2,1,0:T(8,128)S(1)} async-done(((f32[16,8,256]{2,1,0:T(8,128)}), f32[16,8,256]{2,1,0:T(8,128)S(1)}, u32[]{:S(2)}, u32[]{:S(2)}) %all-to-all-start.1) | async-done | bytes 131104 | tf_op jit(solution)/shard_map/all_to_all | solution.py:465
  41.4 1.4 %shard_map.183 = (f32[16,8,384]{2,1,0:T(8,128)S(1)}, f32[256,128]{1,0:T(8,128)S(1)}) custom-call(f32[16,8,256]{2,1,0:T(8,128)S(1)} %all-to-all-done.1.data, f32[256,128]{1,0:T(8,128)S(1)} %get-tuple-element.41.kern, f32[32,128]{1,0:T(8,128)S(1)} %get-tuple-element.42.pack, f32[128,128]{1,0:T(8,128)S(1)} %get-tuple-element.43.ex, ...), custom_call_target="tpu_custom_call" | custom-call | flops 1000000 | bytes 1000000 | tf_op jit(solution)/shard_map/pallas_call | solution.py:459
  42.8 13.3 %all_to_all.31.data = f32[16,8,384]{2,1,0:T(8,128)S(1)} all-to-all(f32[16,8,384]{2,1,0:T(8,128)S(1)} %get-tuple-element.45), channel_id=1, replica_groups=mesh['px'=16,'py'=16] {'px'}, dimensions={0} | all-to-all | bytes 393216 | tf_op jit(solution)/shard_map/all_to_all | solution.py:465
  56.0 0.8 shard_map.184
  56.9 17.6 %all_to_all.32.data = f32[16,8,1152]{2,1,0:T(8,128)S(1)} all-to-all(f32[16,8,1152]{2,1,0:T(8,128)S(1)} %get-tuple-element.49), channel_id=1, replica_groups=mesh['px'=16,'py'=16] {'py'}, dimensions={0} | all-to-all | bytes 1179648 | tf_op jit(solution)/shard_map/all_to_all | solution.py:465
  74.5 0.0 copy-done.1
  74.5 0.0 copy-done.2
  74.5 0.0 copy-done.3
  74.5 3.5 %shard_map.185 = (f32[16,8,384]{2,1,0:T(8,128)S(1)}, bf16[64,8,8,128]{3,2,1,0:T(8,128)(2,1)}) custom-call(f32[16,8,1152]{2,1,0:T(8,128)S(1)} %all_to_all.32.data, bf16[256,256]{1,0:T(8,128)(2,1)S(1)} %copy-done.2, f32[128,128]{1,0:T(8,128)S(1)} %get-tuple-element.50.f3w, f32[8,128]{1,0:T(8,128)S(1)} %get-tuple-element.51.fact_in, ...), custom_call_target="tpu_custom_call" | custom-call | flops 1000000 | bytes 1000000 | tf_op jit(solution)/shard_map/pallas_call | solution.py:459
  78.0 14.0 %all_to_all.33.data = f32[16,8,384]{2,1,0:T(8,128)S(1)} all-to-all(f32[16,8,384]{2,1,0:T(8,128)S(1)} %get-tuple-element.53), channel_id=1, replica_groups=mesh['px'=16,'py'=16] {'px'}, dimensions={0} | all-to-all | bytes 393216 | tf_op jit(solution)/shard_map/all_to_all | solution.py:465
  92.0 0.7 shard_map.186
  92.7 17.0 %all_to_all.34.data = f32[16,8,1408]{2,1,0:T(8,128)S(1)} all-to-all(f32[16,8,1408]{2,1,0:T(8,128)S(1)} %get-tuple-element.54), channel_id=1, replica_groups=mesh['px'=16,'py'=16] {'py'}, dimensions={0} | all-to-all | bytes 1441792 | tf_op jit(solution)/shard_map/all_to_all | solution.py:465
  109.7 3.0 %shard_map.187 = (f32[16,8,8,8,16]{4,3,2,1,0:T(8,128)}, f32[16,64]{1,0:T(8,128)}, f32[16,64]{1,0:T(8,128)}, f32[8,32]{1,0:T(8,128)}) custom-call(f32[16,8,1408]{2,1,0:T(8,128)S(1)} %all_to_all.34.data), custom_call_target="tpu_custom_call" | custom-call | flops 1000000 | bytes 1000000 | tf_op jit(solution)/shard_map/pallas_call | solution.py:459
Async XLA Ops:
  0.6 30.8 %copy-start.6 = (f32[32,8]{0,1:T(8,128)S(1)}, f32[32,8]{0,1:T(8,128)}, u32[]{:S(2)}) copy-start(f32[32,8]{0,1:T(8,128)} %param.20) | copy-start | bytes 3076
  0.6 30.8 %copy-start.5 = (f32[32,8]{0,1:T(8,128)S(1)}, f32[32,8]{0,1:T(8,128)}, u32[]{:S(2)}) copy-start(f32[32,8]{0,1:T(8,128)} %param.19) | copy-start | bytes 3076
  0.7 30.8 %copy-start.4 = (f32[32,8]{0,1:T(8,128)S(1)}, f32[32,8]{0,1:T(8,128)}, u32[]{:S(2)}) copy-start(f32[32,8]{0,1:T(8,128)} %param.18) | copy-start | bytes 3076
  20.8 20.6 %all-to-all-start.1 = ((f32[16,8,256]{2,1,0:T(8,128)}), f32[16,8,256]{2,1,0:T(8,128)S(1)}, u32[]{:S(2)}, u32[]{:S(2)}) async-start(f32[16,8,256]{2,1,0:T(8,128)} %shard_map.181), calls=%async_computation.1 | async-start | bytes 262144 | tf_op jit(solution)/shard_map/all_to_all | solution.py:465
  31.4 2.2 %copy-start = (f32[16,16,8,8,8]{1,4,3,2,0:T(8,128)S(1)}, f32[16,16,8,8,8]{1,4,3,2,0:T(8,128)}, u32[]{:S(2)}) copy-start(f32[16,16,8,8,8]{1,4,3,2,0:T(8,128)} %param.15) | copy-start | bytes 1572868
  33.6 40.9 %copy-start.1 = (bf16[512,64]{1,0:T(8,128)(2,1)S(1)}, bf16[512,64]{1,0:T(8,128)(2,1)}, u32[]{:S(2)}) copy-start(bf16[512,64]{1,0:T(8,128)(2,1)} %constant.14.clone.sy) | copy-start | bytes 196612
  33.6 40.9 %copy-start.2 = (bf16[256,256]{1,0:T(8,128)(2,1)S(1)}, bf16[256,256]{1,0:T(8,128)(2,1)}, u32[]{:S(2)}) copy-start(bf16[256,256]{1,0:T(8,128)(2,1)} %constant.10.clone.zf) | copy-start | bytes 393220
  33.6 40.9 %copy-start.3 = (f32[64,16]{0,1:T(8,128)S(1)}, f32[64,16]{0,1:T(8,128)}, u32[]{:S(2)}) copy-start(f32[64,16]{0,1:T(8,128)} %param.17) | copy-start | bytes 12292

commit v3 on v2

--- a/solution.py
+++ b/solution.py
@@ -58,13 +58,11 @@
                 for r in range(8):
                     sel[t, bh * 16 + mm * 8 + r, r // 4, bh, r % 4, t] = 1.0
     sel = sel.reshape(1024, 128)
-    sy = np.kron(np.eye(64), np.ones((8, 1)))
     return {
         "zf": np.concatenate(split_table(zf), axis=0),
         "yf": np.concatenate(split_table(yf), axis=0),
         "xf": np.stack(split_table(xf)),
         "sel": sel.astype(jnp.bfloat16),
-        "sy": sy.astype(np.float32).astype(jnp.bfloat16),
     }
 
 
@@ -98,6 +96,11 @@
 
 def plane(ref, x):
     return ref[:, x].astype(F32).reshape(512, N).astype(BF16)
+
+
+def sum_y():
+    row, col = lanes((512, 64))
+    return marks(row // 8 == col)
 
 
 def spread(factor, sy):
@@ -109,10 +112,10 @@
     ]
 
 
-def fold_kernel(flow, cot, fin, fout, sy, zf, yf, out, yout, fields, tin, tout, tsy, tzf, work, sems):
+def fold_kernel(flow, cot, fin, fout, zf, yf, out, yout, tout, fields, tin, tzf, work, sems):
     small = [
         pltpu.make_async_copy(src, dst, sems.at[8 + i])
-        for i, (src, dst) in enumerate(((fin, tin), (fout, tout), (sy, tsy), (zf, tzf)))
+        for i, (src, dst) in enumerate(((fin, tin), (fout, tout), (zf, tzf)))
     ]
     for copy in small:
         copy.start()
@@ -129,8 +132,9 @@
     get_yf.start()
     for copy in small:
         copy.wait()
+    sy = sum_y()
     for f, factor in enumerate((tin, tout)):
-        w = jnp.concatenate(spread(factor[...], tsy[...]), axis=0)
+        w = jnp.concatenate(spread(factor[...], sy), axis=0)
         for copy in large[4 * f : 4 * f + 4]:
             copy.wait()
         for pair in range(4):
@@ -165,9 +169,19 @@
     return jnp.where(cond, 1.0, 0.0).astype(BF16)
 
 
-def prep_kernel(core, f1t, f2t, f3t, xf, kern, flat, xbuf, pack, ex, f2w, f3w, sem):
-    get = pltpu.make_async_copy(xf, xbuf, sem)
-    get.start()
+def prep_kernel(
+    f1h, f2h, f3h, core, xf, kern, flat, xbuf, pack, ex, f2w, f3w, f1t, f2t, f3t, cbuf, sems
+):
+    small = [
+        pltpu.make_async_copy(src, dst, sems.at[i])
+        for i, (src, dst) in enumerate(((f1h, f1t), (f2h, f2t), (f3h, f3t)))
+    ]
+    loads = [pltpu.make_async_copy(core.at[a], cbuf.at[a], sems.at[4 + a]) for a in range(16)]
+    get = pltpu.make_async_copy(xf, xbuf, sems.at[3])
+    for copy in small + loads + [get]:
+        copy.start()
+    for copy in small:
+        copy.wait()
     px, py = lax.axis_index("px"), lax.axis_index("py")
     row, lane = lanes((32, N))
     f1 = pick(f1t[...], marks(row == lane % 32))
@@ -181,8 +195,6 @@
     wide = mul(parts[0], spread_r, TN) + mul(parts[1], spread_r, TN) + mul(parts[2], spread_r, TN)
     row, lane = lanes((N, N))
     ex[...] = jnp.where(row // 32 == lane // 8, wide, 0.0)
-    for a in range(16):
-        flat[a * 16 : (a + 1) * 16, :] = core[a].T
     w = jnp.concatenate(
         [f1[r : r + 1] * f2[s : s + 1] * f3 for r in range(8) for s in range(8)], axis=0
     )
@@ -194,6 +206,9 @@
         f2w[d * 8 : d * 8 + 8] = wide2[:, d * N : (d + 1) * N]
         f3w[d * 8 : d * 8 + 8] = wide3[:, d * N : (d + 1) * N]
     wh, wl = split(w)
+    for a in range(16):
+        loads[a].wait()
+        flat[a * 16 : (a + 1) * 16, :] = cbuf[a].T
     ch, cl = split(flat[...])
     kern[...] = mul(ch, wh) + mul(cl, wh) + mul(ch, wl)
     get.wait()
@@ -284,56 +299,7 @@
         out[2 * s + 1, :, 1024:1152] = acc
 
 
-def space_kernel(
-    data, zf, f3w, fact_in, sy, fout, flow, cot, sel, out, result, fields, vout, obuf, pacc, tsel, sems
-):
-    loads = []
-    for f, field in enumerate((flow, cot)):
-        for part in range(4):
-            rows = pl.ds(16 * part, 16)
-            load = pltpu.make_async_copy(
-                field.at[rows], fields.at[f, rows], sems.at[4 * f + part]
-            )
-            load.start()
-            loads.append(load)
-    get_sel = pltpu.make_async_copy(sel, tsel, sems.at[8])
-    get_sel.start()
-    zh, zl = zf[:128], zf[128:]
-    for g in range(4):
-        v = data[:, :, g * 256 : (g + 1) * 256].reshape(128, 256)
-        hi, lo = split(v)
-        r = mul(hi, zh, TN) + mul(lo, zh, TN) + mul(hi, zl, TN)
-        rh, rl = split(r)
-        for x in range(8):
-            for f in range(2):
-                for y2 in range(2):
-                    row = (2 * g + y2) * 16
-                    src = slice(x * 32 + f * 16, x * 32 + f * 16 + 16)
-                    cols = slice(y2 * N, (y2 + 1) * N)
-                    vout[f, row : row + 16, x * N : (x + 1) * N] = rh[src, cols]
-                    vout[f, 128 + row : 128 + row + 16, x * N : (x + 1) * N] = rl[src, cols]
-    brow, bcol = lanes((16, N))
-    repeat = marks(brow == bcol % 16)
-    orow, ocol = lanes((512, N))
-    wide = [
-        jnp.where(orow % 8 == ocol // 16, mul(sy[...], mul(part, repeat, TN).astype(BF16)), 0.0)
-        for part in split(fout[...])
-    ]
-    hi, lo = wide[0].astype(BF16), wide[1].astype(BF16)
-    w = jnp.concatenate([hi, hi, lo], axis=1)
-    for pair in range(4):
-        cols = slice(pair * 256, (pair + 1) * 256)
-        hi = vout[0, 0:128, cols]
-        lo = vout[0, 128:256, cols]
-        u = mul(w, jnp.concatenate([hi, lo, hi], axis=0))
-        for x2 in range(2):
-            obuf[:, 2 * pair + x2] = u[:, x2 * N : (x2 + 1) * N].reshape(64, 8, N).astype(BF16)
-    puts = []
-    for part in range(4):
-        rows = pl.ds(16 * part, 16)
-        put = pltpu.make_async_copy(obuf.at[rows], result.at[rows], sems.at[9 + part])
-        put.start()
-        puts.append(put)
+def core_tile(data, f3w, fact_in, get_sel, tsel):
     fact = data[0, :, 1024:1152]
     for d in range(1, 16):
         fact = fact + data[d, :, 1024:1152]
@@ -349,46 +315,69 @@
     core = jnp.where(lane // 64 == lax.axis_index("py") % 2, core, 0.0)
     core = core + pltpu.roll(core, 64, 1)
     fact = jnp.where((lane == 66) | (lane == 67), fact_in[...], fact)
-    last = jnp.where(lane < 64, core, fact)
+    return jnp.where(lane < 64, core, fact)
+
+
+def space_kernel(
+    data, zf, f3w, fact_in, flow, cot, sel, out, vfirst, second, vsecond, tsel, sems
+):
+    sy = sum_y()
+    vout = (vfirst, vsecond)
+    get_sel = pltpu.make_async_copy(sel, tsel, sems.at[8])
+    get_sel.start()
+    loads = []
+    for part in range(4):
+        rows = pl.ds(16 * part, 16)
+        load = pltpu.make_async_copy(cot.at[rows], second.at[rows], sems.at[part])
+        load.start()
+        loads.append(load)
+    zh, zl = zf[:128], zf[128:]
+    for g in range(4):
+        v = data[:, :, g * 256 : (g + 1) * 256].reshape(128, 256)
+        hi, lo = split(v)
+        r = mul(hi, zh, TN) + mul(lo, zh, TN) + mul(hi, zl, TN)
+        rh, rl = split(r)
+        for x in range(8):
+            for f in range(2):
+                for y2 in range(2):
+                    row = (2 * g + y2) * 16
+                    src = slice(x * 32 + f * 16, x * 32 + f * 16 + 16)
+                    cols = slice(y2 * N, (y2 + 1) * N)
+                    vout[f][row : row + 16, x * N : (x + 1) * N] = rh[src, cols]
+                    vout[f][128 + row : 128 + row + 16, x * N : (x + 1) * N] = rl[src, cols]
     ri, ci = lanes((128, 512))
     same = ri // 16 == ci % 8
     res = []
-    for f in range(2):
-        field = fields.at[f]
-        for load in loads[4 * f : 4 * f + 4]:
+    for f, field in enumerate((flow, second)):
+        for load in loads if f else ():
             load.wait()
-        for pair in range(4):
-            u = jnp.concatenate([plane(field, 2 * pair), plane(field, 2 * pair + 1)], axis=1)
-            part = mul(vout[1 - f, :, pair * 256 : (pair + 1) * 256], u, NT)
-            if pair == 0:
-                pacc[...] = part
-            else:
-                pacc[...] += part
-        p = jnp.where(same, pacc[:128] + pacc[128:], 0.0)
+        u = jnp.concatenate([plane(field, x) for x in range(8)], axis=1)
+        part = mul(vout[1 - f][...], u, NT)
+        p = jnp.where(same, part[:128] + part[128:], 0.0)
         q = p[0:16]
         for yy in range(1, 8):
             q = q + p[yy * 16 : yy * 16 + 16]
-        res.append(pick(q, sy[...]))
+        res.append(pick(q, sy))
+        if f == 0:
+            last = core_tile(data, f3w, fact_in, get_sel, tsel)
     both = jnp.concatenate(res, axis=1)
     row = jnp.concatenate([both[0:8], both[8:16], last], axis=1)
     for d in range(16):
         out[d] = row
-    for put in puts:
-        put.wait()
-
-
-def gather_kernel(data, out, g1, g2):
+
+
+def gather_kernel(data, out, sums):
     total = data[0]
     for d in range(1, 16):
         total = total + data[d]
     fact = total[:, 256:384]
-    g1[...] = pltpu.roll(fact, N - 96, 1)[:, :32]
+    first = pltpu.roll(fact, N - 96, 1)
     lane = lax.broadcasted_iota(jnp.int32, (8, N), 1)
     second = jnp.zeros((8, N), F32)
     for d in range(16):
-        moved = pltpu.roll(data[d, :, 256:384], (2 * d - 64) % N, 1)
-        second = jnp.where(lane // 2 == d, moved, second)
-    g2[...] = second[:, :32]
+        moved = pltpu.roll(data[d, :, 256:384], (2 * d - 32) % N, 1)
+        second = jnp.where(lane // 2 == d + 16, moved, second)
+    sums[...] = jnp.where(lane < 32, first, second)
     tiles = []
     for bh in range(2):
         for q in range(4):
@@ -399,36 +388,97 @@
                 moved = pltpu.roll(moved, shift, 1) if shift else moved
                 tile = jnp.where(lane // 32 == i, moved, tile)
             tiles.append(tile)
-    row = jnp.concatenate([total[:, 0:256]] + tiles + [fact], axis=1)
+    rows = [
+        jnp.concatenate(
+            [total[:, h * N : (h + 1) * N]]
+            + tiles[2 * h : 2 * h + 2]
+            + tiles[2 * h + 4 : 2 * h + 6]
+            + [fact],
+            axis=1,
+        )
+        for h in range(2)
+    ]
     for d in range(16):
-        out[d] = row
-
-
-def final_kernel(data, core, gin, gout, g3, buf, sems):
+        out[d] = rows[d % 2]
+
+
+def write_half(data, core, buf, sems, which):
     sends = []
-    for q in range(4):
+    for q in range(2):
         for d in range(16):
-            lo, hi = 256 + q * N, 768 + q * N
+            lo, hi = N + q * N, 3 * N + q * N
             c = jnp.concatenate([data[d, :, lo : lo + N], data[d, :, hi : hi + N]], axis=0)
             rows = slice(d % 2 * 4, d % 2 * 4 + 4)
             buf[4 * q : 4 * q + 4, rows, d // 2] = c.T.reshape(4, 4, 8, 16)
-        part = pl.ds(4 * q, 4)
-        send = pltpu.make_async_copy(buf.at[part], core.at[part], sems.at[q])
+        send = pltpu.make_async_copy(
+            buf.at[pl.ds(4 * q, 4)], core.at[pl.ds(8 * which + 4 * q, 4)], sems.at[q]
+        )
         send.start()
         sends.append(send)
-    total = data[0, :, 0:256]
+    return sends
+
+
+def expand(v, fout, field, obuf, sems):
+    row, col = lanes((16, N))
+    repeat = marks(row == col % 16)
+    choose = sum_y()
+    row, col = lanes((512, N))
+    hi, lo = [
+        jnp.where(row % 8 == col // 16, mul(choose, mul(part, repeat, TN).astype(BF16)), 0.0).astype(BF16)
+        for part in split(fout[...])
+    ]
+    w = jnp.concatenate([hi, hi, lo], axis=1)
+    parts = jnp.concatenate([v[0:128], v[128:256], v[0:128]], axis=0)
+    puts = []
+    for q in range(4):
+        u = mul(w[q * 128 : (q + 1) * 128], parts)
+        for x in range(8):
+            obuf[q * 16 : (q + 1) * 16, x] = u[:, x * N : (x + 1) * N].reshape(16, 8, N).astype(BF16)
+        put = pltpu.make_async_copy(
+            obuf.at[pl.ds(16 * q, 16)], field.at[pl.ds(16 * q, 16)], sems.at[2 + q]
+        )
+        put.start()
+        puts.append(put)
+    return puts
+
+
+def own_kernel(data, v, fout, sums, core, field, g1, g2, g3, mine, buf, obuf, gbuf, sems):
+    sends = write_half(data, core, buf, sems, lax.axis_index("py") % 2)
+    total = data[0, :, 0:N]
     for d in range(1, 16):
-        total = total + data[d, :, 0:256]
-    gin[0:8] = total[:, 0:64]
-    gin[8:16] = total[:, 128:192]
-    gout[0:8] = pltpu.roll(total[:, 0:128], 64, 1)[:, :64]
-    gout[8:16] = pltpu.roll(total[:, 128:256], 64, 1)[:, :64]
-    lane = lax.broadcasted_iota(jnp.int32, (8, N), 1)
+        total = total + data[d, :, 0:N]
+    mine[...] = total
+    lane = lanes((8, N))[1]
     third = jnp.zeros((8, N), F32)
     for d in range(16):
-        moved = pltpu.roll(data[d, :, 1280:1408], (2 * d - 66) % N, 1)
+        moved = pltpu.roll(data[d, :, 640:768], (2 * d - 66) % N, 1)
         third = jnp.where(lane // 2 == d, moved, third)
-    g3[...] = third[:, :32]
+    gbuf[0] = sums[:, :32]
+    gbuf[1] = sums[:, 32:64]
+    gbuf[2] = third[:, :32]
+    for i, dst in enumerate((g1, g2, g3)):
+        send = pltpu.make_async_copy(gbuf.at[i], dst, sems.at[6 + i])
+        send.start()
+        sends.append(send)
+    sends += expand(v, fout, field, obuf, sems)
+    for send in sends:
+        send.wait()
+
+
+def other_kernel(data, mine, core_in, core, gin, gout, buf, gbuf, sems):
+    h = lax.axis_index("py") % 2
+    sends = write_half(data, core, buf, sems, 1 - h)
+    total = data[0, :, 0:N]
+    for d in range(1, 16):
+        total = total + data[d, :, 0:N]
+    own = mine[...]
+    for i, rows in enumerate((jnp.where(h == 0, own, total), jnp.where(h == 0, total, own))):
+        gbuf[0, 8 * i : 8 * i + 8] = rows[:, :64]
+        gbuf[1, 8 * i : 8 * i + 8] = pltpu.roll(rows, 64, 1)[:, :64]
+    for i, dst in enumerate((gin, gout)):
+        send = pltpu.make_async_copy(gbuf.at[i], dst, sems.at[2 + i])
+        send.start()
+        sends.append(send)
     for send in sends:
         send.wait()
 
@@ -438,7 +488,7 @@
 DMA = pltpu.SemaphoreType.DMA
 
 
-def call(kernel, ins, outs, scratch=(), flops=1_000_000, vmem=12):
+def call(kernel, ins, outs, scratch=(), flops=1_000_000, vmem=12, aliases=None):
     shapes = [
         pltpu.HBM(*o[:2]) if len(o) > 2 and o[2] is HB
         else jax.ShapeDtypeStruct(*o)
@@ -450,6 +500,7 @@
         in_specs=[VM] * ins[0] + [HB] * ins[1],
         out_specs=[o[2] if len(o) > 2 else VM for o in outs],
         scratch_shapes=list(scratch),
+        input_output_aliases=aliases or {},
         cost_estimate=pl.CostEstimate(flops=flops, bytes_accessed=1_000_000, transcendentals=0),
         compiler_params=pltpu.CompilerParams(vmem_limit_bytes=vmem * 1024 * 1024),
     )
@@ -469,27 +520,25 @@
     tab = {name: jnp.asarray(value) for name, value in tables().items()}
     fin, fout = in_factor.T, out_factor.T
 
-    o1, yf = call(
+    o1, yf, fout = call(
         fold_kernel,
-        (0, 7),
-        [((16, 8, 1024), F32), ((256, 512), BF16)],
+        (0, 6),
+        [((16, 8, 1024), F32), ((256, 512), BF16), ((16, 64), F32)],
         [
             pltpu.VMEM((2, 64, 8, 8, N), BF16),
             pltpu.VMEM((16, 64), F32),
-            pltpu.VMEM((16, 64), F32),
-            pltpu.VMEM((512, 64), BF16),
             pltpu.VMEM((256, 256), BF16),
             pltpu.VMEM((4, 256, 256), F32),
             DMA((13,)),
         ],
-    )(flow, cot, fin, fout, tab["sy"], tab["zf"], tab["yf"])
+    )(flow, cot, fin, fout, tab["zf"], tab["yf"])
     r1 = exchange(o1, "py")
     r1, core, first, second, third = lax.optimization_barrier((r1, core, first, second, third))
     f1t, f2t, f3t = first.T, second.T, third.T
     core_t = core.transpose(0, 2, 3, 4, 1).reshape(16, 512, 16)
     kern, flat, xf, pack, ex, f2w, f3w = call(
         prep_kernel,
-        (4, 1),
+        (0, 5),
         [
             ((256, N), F32),
             ((256, 512), F32),
@@ -499,9 +548,9 @@
             ((N, N), F32),
             ((N, N), F32),
         ],
-        [DMA],
+        [pltpu.VMEM((8, 32), F32)] * 3 + [pltpu.VMEM((16, 512, 16), F32), DMA((20,))],
         flops=100_000_000,
-    )(core_t, f1t, f2t, f3t, tab["xf"])
+    )(f1t, f2t, f3t, core_t, tab["xf"])
     o2 = call(y_kernel, (2, 0), [((16, 8, 256), F32)])(r1, yf)[0]
     r2 = exchange(o2, "px")
     o3, gk = call(mode_kernel, (5, 0), [((16, 8, 384), F32), ((256, N), F32)])(
@@ -512,30 +561,39 @@
         r3, yf, f2w, gk, flat, pack
     )
     r4 = exchange(o4, "py")
-    o5, field = call(
+    o5, v = call(
         space_kernel,
-        (6, 3),
-        [((16, 8, 384), F32), ((64, 8, 8, N), BF16, HB)],
+        (5, 2),
+        [((16, 8, 384), F32), ((256, 1024), BF16)],
         [
-            pltpu.VMEM((2, 64, 8, 8, N), BF16),
-            pltpu.VMEM((2, 256, 1024), BF16),
             pltpu.VMEM((64, 8, 8, N), BF16),
-            pltpu.VMEM((256, 512), F32),
+            pltpu.VMEM((256, 1024), BF16),
             pltpu.VMEM((1024, N), BF16),
-            DMA((13,)),
+            DMA((9,)),
         ],
-    )(r4, tab["zf"], f3w, fact, tab["sy"], fout, flow, cot, tab["sel"])
+    )(r4, tab["zf"], f3w, fact, flow, cot, tab["sel"])
     r5 = exchange(o5, "px")
-    o6, g1, g2 = call(
-        gather_kernel, (1, 0), [((16, 8, 1408), F32), ((8, 32), F32), ((8, 32), F32)]
-    )(r5)
+    o6, sums = call(gather_kernel, (1, 0), [((16, 8, 768), F32), ((8, N), F32)])(r5)
     r6 = exchange(o6, "py")
-    gcore, gin, gout, g3 = call(
-        final_kernel,
-        (1, 0),
-        [((16, 8, 8, 8, 16), F32, HB), ((16, 64), F32), ((16, 64), F32), ((8, 32), F32)],
-        [pltpu.VMEM((16, 8, 8, 8, 16), F32), DMA((4,))],
-    )(r6)
+    swapped = lax.ppermute(r6, "py", [(i, i ^ 1) for i in range(16)])
+    whole = ((16, 8, 8, 8, 16), F32, HB)
+    half = pltpu.VMEM((8, 8, 8, 8, 16), F32)
+    small = ((8, 32), F32, HB)
+    gcore, field, g1, g2, g3, mine = call(
+        own_kernel,
+        (4, 0),
+        [whole, ((64, 8, 8, N), BF16, HB), small, small, small, ((8, N), F32)],
+        [half, pltpu.VMEM((64, 8, 8, N), BF16), pltpu.VMEM((3, 8, 32), F32), DMA((9,))],
+        flops=100_000_000,
+    )(r6, v, fout, sums)
+    small = ((16, 64), F32, HB)
+    gcore, gin, gout = call(
+        other_kernel,
+        (2, 1),
+        [whole, small, small],
+        [half, pltpu.VMEM((2, 16, 64), F32), DMA((4,))],
+        aliases={2: 0},
+    )(swapped, mine, gcore)
     return (field, gcore.transpose(0, 4, 1, 2, 3), gin.T, gout.T, g1.T, g2.T, g3.T)
 
 

time: 113 us -> 110 us (0.973)
  blocking collectives: 78.2 us -> 74.4 us
  local copies, waits for them, and re-layouts: 2.21 us -> 0.01 us
  Pallas kernels: 14.8 us -> 16.3 us
    all_to_all x5, blocking collectives: 78.2 us -> 74.4 us  [exchange(): return lax.all_to_all(v, axis, split_axis=0, concat_axis=0, tiled=True)]
    unnamed x14 -> x4, local copies, waits for them, and re-layouts: 2.21 us -> 0.01 us
    pallas_call x8 -> x9, Pallas kernels: 14.8 us -> 16.3 us  [placed(): return run(*args[:ins[0]], *far)]
  transfers between devices with their start and end apart: 1 -> 2, of which waited for: 1 -> 1; matrix products, arithmetic and copies ran while one was open for 0% -> 0% of each run, Pallas kernels for 1% -> 5%
where the time goes in v3:
time: 110 us; the launch traced here: 109 us
  blocking collectives  74.4 us (68%)
  Pallas kernels  16.3 us (15%)
  starting transfers between devices  11.3 us (10%)
  waiting for transfers between devices  6.39 us (6%)
    all_to_all x5, blocking collectives, exchange(): return lax.all_to_all(v, axis, split_axis=0, concat_axis=0, tiled=True)  74.4 us
    pallas_call x9, Pallas kernels, placed(): return run(*args[:ins[0]], *far)  16.3 us
    all_to_all x1, starting transfers between devices, exchange(): return lax.all_to_all(v, axis, split_axis=0, concat_axis=0, tiled=True)  10.6 us
    all_to_all x1, waiting for transfers between devices, exchange(): return lax.all_to_all(v, axis, split_axis=0, concat_axis=0, tiled=True)  6.39 us
  transfers between devices with their start and end apart: 2, of which 1 were waited for; matrix products, arithmetic and copies ran while one was open for 0% of the time, Pallas kernels for 5%

profile of v3, /device:TPU:1, one launch (start us, length us, event | category | flops | bytes accessed | tf_op | source)
XLA Modules:
  0.0 109.1 jit_solution(15798124990670128583)
XLA Ops:
  0.6 2.7 %shard_map.171 = (f32[16,8,1024]{2,1,0:T(8,128)S(1)}, bf16[256,512]{1,0:T(8,128)(2,1)S(1)}, f32[16,64]{1,0:T(8,128)S(1)}) custom-call(bf16[64,8,8,128]{3,2,1,0:T(8,128)(2,1)} %flow.3, bf16[64,8,8,128]{3,2,1,0:T(8,128)(2,1)} %cot.3, f32[16,64]{1,0:T(8,128)} %bitcast.16, f32[16,64]{1,0:T(8,128)} %bitcast.17, bf16[256,256]{1,0:T(8,128)(2,1)} %constant.8.clone.zf, ...), custom_call_target="tpu_custom_call" | custom-call | flops 1000000 | bytes 1000000 | tf_op jit(solution)/shard_map/pallas_call | solution.py:510
  3.4 16.3 %all_to_all.30.data = f32[16,8,1024]{2,1,0:T(8,128)S(1)} all-to-all(f32[16,8,1024]{2,1,0:T(8,128)S(1)} %get-tuple-element.39), channel_id=1, replica_groups=mesh['px'=16,'py'=16] {'py'}, dimensions={0} | all-to-all | bytes 1048576 | tf_op jit(solution)/shard_map/all_to_all | solution.py:516
  19.7 0.9 shard_map.172
  20.6 10.6 %all-to-all-start.1 = ((f32[16,8,256]{2,1,0:T(8,128)}), f32[16,8,256]{2,1,0:T(8,128)S(1)}, u32[]{:S(2)}, u32[]{:S(2)}) async-start(f32[16,8,256]{2,1,0:T(8,128)} %shard_map.172), calls=%async_computation.1 | async-start | bytes 262144 | tf_op jit(solution)/shard_map/all_to_all | solution.py:516
  31.3 0.0 copy-start
  31.3 0.0 copy-start.1
  31.3 3.6 %shard_map.173 = (f32[256,128]{1,0:T(8,128)S(1)}, f32[256,512]{1,0:T(8,128)S(1)}, bf16[2,1024,256]{2,1,0:T(8,128)(2,1)S(1)}, f32[32,128]{1,0:T(8,128)S(1)}, f32[...) custom-call(f32[8,32]{1,0:T(8,128)} %bitcast.18, f32[8,32]{1,0:T(8,128)} %bitcast.19, ...), custom_call_target="tpu_custom_call" | custom-call | flops 100000000 | bytes 1000000 | tf_op jit(solution)/shard_map/pallas_call | solution.py:510
  34.9 6.4 %all-to-all-done.1.data = f32[16,8,256]{2,1,0:T(8,128)S(1)} async-done(((f32[16,8,256]{2,1,0:T(8,128)}), f32[16,8,256]{2,1,0:T(8,128)S(1)}, u32[]{:S(2)}, u32[]{:S(2)}) %all-to-all-start.1) | async-done | bytes 131104 | tf_op jit(solution)/shard_map/all_to_all | solution.py:516
  41.2 1.4 %shard_map.174 = (f32[16,8,384]{2,1,0:T(8,128)S(1)}, f32[256,128]{1,0:T(8,128)S(1)}) custom-call(f32[16,8,256]{2,1,0:T(8,128)S(1)} %all-to-all-done.1.data, f32[256,128]{1,0:T(8,128)S(1)} %get-tuple-element.46.kern, f32[32,128]{1,0:T(8,128)S(1)} %get-tuple-element.47.pack, f32[128,128]{1,0:T(8,128)S(1)} %get-tuple-element.48.ex, ...), custom_call_target="tpu_custom_call" | custom-call | flops 1000000 | bytes 1000000 | tf_op jit(solution)/shard_map/pallas_call | solution.py:510
  42.7 13.4 %all_to_all.31.data = f32[16,8,384]{2,1,0:T(8,128)S(1)} all-to-all(f32[16,8,384]{2,1,0:T(8,128)S(1)} %get-tuple-element.50), channel_id=1, replica_groups=mesh['px'=16,'py'=16] {'px'}, dimensions={0} | all-to-all | bytes 393216 | tf_op jit(solution)/shard_map/all_to_all | solution.py:516
  56.0 0.8 shard_map.175
  56.9 17.5 %all_to_all.32.data = f32[16,8,1152]{2,1,0:T(8,128)S(1)} all-to-all(f32[16,8,1152]{2,1,0:T(8,128)S(1)} %get-tuple-element.54), channel_id=1, replica_groups=mesh['px'=16,'py'=16] {'py'}, dimensions={0} | all-to-all | bytes 1179648 | tf_op jit(solution)/shard_map/all_to_all | solution.py:516
  74.4 0.0 copy-done
  74.4 0.0 copy-done.1
  74.4 2.7 %shard_map.176 = (f32[16,8,384]{2,1,0:T(8,128)S(1)}, bf16[256,1024]{1,0:T(8,128)(2,1)S(1)}) custom-call(f32[16,8,1152]{2,1,0:T(8,128)S(1)} %all_to_all.32.data, bf16[256,256]{1,0:T(8,128)(2,1)S(1)} %copy-done.1, f32[128,128]{1,0:T(8,128)S(1)} %get-tuple-element.55.f3w, f32[8,128]{1,0:T(8,128)S(1)} %get-tuple-element.56.fact_in, ...), custom_call_target="tpu_custom_call" | custom-call | flops 1000000 | bytes 1000000 | tf_op jit(solution)/shard_map/pallas_call | solution.py:510
  77.1 14.0 %all_to_all.33.data = f32[16,8,384]{2,1,0:T(8,128)S(1)} all-to-all(f32[16,8,384]{2,1,0:T(8,128)S(1)} %get-tuple-element.57), channel_id=1, replica_groups=mesh['px'=16,'py'=16] {'px'}, dimensions={0} | all-to-all | bytes 393216 | tf_op jit(solution)/shard_map/all_to_all | solution.py:516
  91.2 0.1 shard_map.177
  91.3 13.2 %all_to_all.34.data = f32[16,8,768]{2,1,0:T(8,128)S(1)} all-to-all(f32[16,8,768]{2,1,0:T(8,128)S(1)} %get-tuple-element.58), channel_id=1, replica_groups=mesh['px'=16,'py'=16] {'py'}, dimensions={0} | all-to-all | bytes 786432 | tf_op jit(solution)/shard_map/all_to_all | solution.py:516
  104.5 0.6 collective-permute-start
  105.2 2.2 %shard_map.178 = (f32[16,8,8,8,16]{4,3,2,1,0:T(8,128)}, bf16[64,8,8,128]{3,2,1,0:T(8,128)(2,1)}, f32[8,32]{1,0:T(8,128)}, f32[8,32]{1,0:T(8,128)}, f32[8,32]{1,0:T(8,128)}, /*index=5*/f32[8,128]{1,0:T(8,128)S(1)}) custom-call(f32[16,8,768]{2,1,0:T(8,128)S(1)} %all_to_all.34.data, bf16[256,1024]{1,0:T(8,128)(2,1)S(1)} %get-tuple-element.59.v, ...), custom_call_target="tpu_custom_call" | custom-call | flops 100000000 | bytes 1000000 | tf_op jit(solution)/shard_map/pallas_call | solution.py:510
  107.4 0.0 collective-permute-done.data
  107.4 1.7 %shard_map.179 = (f32[16,8,8,8,16]{4,3,2,1,0:T(8,128)}, f32[16,64]{1,0:T(8,128)}, f32[16,64]{1,0:T(8,128)}) custom-call(f32[16,8,768]{2,1,0:T(8,128)S(1)} %collective-permute-done.data, f32[8,128]{1,0:T(8,128)S(1)} %get-tuple-element.63.mine, f32[16,8,8,8,16]{4,3,2,1,0:T(8,128)} %get-tuple-element.64.core_in), custom_call_target="tpu_custom_call", output_to_operand_aliasing={{0}: (2, {})} | custom-call | flops 1000000 | bytes 1000000 | tf_op jit(solution)/shard_map/pallas_call | solution.py:510
Async XLA Ops:
  20.6 20.6 %all-to-all-start.1 = ((f32[16,8,256]{2,1,0:T(8,128)}), f32[16,8,256]{2,1,0:T(8,128)S(1)}, u32[]{:S(2)}, u32[]{:S(2)}) async-start(f32[16,8,256]{2,1,0:T(8,128)} %shard_map.172), calls=%async_computation.1 | async-start | bytes 262144 | tf_op jit(solution)/shard_map/all_to_all | solution.py:516
  31.3 43.1 %copy-start = (bf16[64,8,8,128]{3,2,1,0:T(8,128)(2,1)S(1)}, bf16[64,8,8,128]{3,2,1,0:T(8,128)(2,1)}, u32[]{:S(2)}) copy-start(bf16[64,8,8,128]{3,2,1,0:T(8,128)(2,1)} %flow.3) | copy-start | bytes 3145732
  31.3 43.1 %copy-start.1 = (bf16[256,256]{1,0:T(8,128)(2,1)S(1)}, bf16[256,256]{1,0:T(8,128)(2,1)}, u32[]{:S(2)}) copy-start(bf16[256,256]{1,0:T(8,128)(2,1)} %constant.8.clone.zf) | copy-start | bytes 393220
  104.5 2.9 %collective-permute-start = (f32[16,8,768]{2,1,0:T(8,128)S(1)}, f32[16,8,768]{2,1,0:T(8,128)S(1)}, u32[]{:S(2)}, u32[]{:S(2)}) collective-permute-start(f32[16,8,768]{2,1,0:T(8,128)S(1)} %all_to_all.34.data), channel_id=1, source_target_pairs={{0,1},{1,0},{2,3},{3,2},{4,5},{5,4},{6,7},{7,6},{8,9},{9,8},{10,11... | collective-permute-start | bytes 1179656 | tf_op jit(solution)/shard_map/ppermute | solution.py:578

commit v4 on v3

--- a/solution.py
+++ b/solution.py
@@ -90,8 +90,18 @@
 
 
 def pick(v, table):
-    hi, mid, lo = split3(v)
-    return mul(hi, table) + mul(mid, table) + mul(lo, table)
+    rows = v.shape[0]
+    parts = jnp.concatenate([part.astype(F32) for part in split3(v)], axis=0).astype(BF16)
+    both = mul(parts, table)
+    return both[:rows] + both[rows : 2 * rows] + both[2 * rows :]
+
+
+def stacked(v, hi, lo, dims=NN):
+    axis = 1 if dims is TN else 0
+    vh, vl = split(v)
+    both = mul(jnp.concatenate([vh, vl], axis=axis), hi, dims)
+    half = both.shape[0] // 2
+    return both[:half] + both[half:] + mul(vh, lo, dims)
 
 
 def plane(ref, x):
@@ -122,21 +132,16 @@
     get_yf = pltpu.make_async_copy(yf, yout, sems.at[12])
     large = []
     for f, field in enumerate((flow, cot)):
-        for part in range(4):
-            rows = pl.ds(16 * part, 16)
-            copy = pltpu.make_async_copy(
-                field.at[rows], fields.at[f, rows], sems.at[4 * f + part]
-            )
-            copy.start()
-            large.append(copy)
+        copy = pltpu.make_async_copy(field, fields.at[f], sems.at[f])
+        copy.start()
+        large.append(copy)
     get_yf.start()
     for copy in small:
         copy.wait()
     sy = sum_y()
     for f, factor in enumerate((tin, tout)):
         w = jnp.concatenate(spread(factor[...], sy), axis=0)
-        for copy in large[4 * f : 4 * f + 4]:
-            copy.wait()
+        large[f].wait()
         for pair in range(4):
             u = jnp.concatenate(
                 [plane(fields.at[f], 2 * pair), plane(fields.at[f], 2 * pair + 1)], axis=1
@@ -144,7 +149,7 @@
             both = mul(w, u)
             v = both[:128] + both[128:]
             for x2 in range(2):
-                row = ((2 * pair + x2) * 2 + f) * 16
+                row = f * 128 + (2 * pair + x2) * 16
                 for yy in range(8):
                     work[yy // 2, row : row + 16, (yy % 2) * N : (yy % 2 + 1) * N] = v[
                         yy * 16 : yy * 16 + 16, x2 * N : (x2 + 1) * N
@@ -216,10 +221,12 @@
 
 def mode_kernel(data, kern, pack, ex, xf, out, gk):
     v = data[...].reshape(128, 256)
-    t = jnp.concatenate([v[:, :128].T, v[:, 128:].T], axis=0)
-    t = jnp.concatenate([t[x * 32 : (x + 1) * 32] for x in range(8)], axis=1)
-    hi, lo = split(t)
-    s = mul(hi, xf[0]) + mul(lo, xf[0]) + mul(hi, xf[1])
+    t = [v[:, :128].T, v[:, 128:].T]
+    t = jnp.concatenate(
+        [jnp.concatenate([part[x * 16 : (x + 1) * 16] for part in t], axis=0) for x in range(8)],
+        axis=1,
+    )
+    s = stacked(t, xf[0], xf[1])
     wt = pack[24:25]
     lift = [s[:16, q * N : (q + 1) * N] for q in range(2)]
     back = [s[16:, q * N : (q + 1) * N] * wt for q in range(2)]
@@ -241,14 +248,16 @@
     n = jnp.concatenate(
         [jnp.concatenate([mixed[q] * wt, low[q]], axis=0) for q in range(2)], axis=1
     )
-    hi, lo = split(n)
-    u = mul(hi, xf[0], NT) + mul(lo, xf[0], NT) + mul(hi, xf[1], NT)
-    u = jnp.concatenate([u[:, x * N : (x + 1) * N] for x in range(8)], axis=0)
-    u = jnp.concatenate([u[:128].T, u[128:].T], axis=1)
+    u = stacked(n, xf[0], xf[1], NT)
+    u = jnp.concatenate(
+        [
+            jnp.concatenate([u[f * 16 : f * 16 + 16, x * N : (x + 1) * N] for x in range(8)], axis=0).T
+            for f in range(2)
+        ],
+        axis=1,
+    )
     out[:, :, 0:256] = u.reshape(16, 8, 256)
-    gh, gl = split(gall)
-    eh, el = split(ex[...])
-    gj = mul(gh, eh) + mul(gl, eh) + mul(gh, el)
+    gj = stacked(gall, *split(ex[...]))
     gj = gj.reshape(16, 2, 8, N)
     for a in range(16):
         out[a, :, 256:384] = gj[a, 0] + pltpu.roll(gj[a, 1], 64, 1)
@@ -257,7 +266,7 @@
 def factor_grads(gk, flat, pack):
     gh, gl = split(gk[...])
     ch, cl = split(flat[...])
-    gw = mul(ch, gh, TN) + mul(cl, gh, TN) + mul(ch, gl, TN)
+    gw = mul(jnp.concatenate([ch, cl], axis=0), jnp.concatenate([gh, gh], axis=0), TN) + mul(ch, gl, TN)
     f1, f2, f3 = pack[0:8], pack[8:16], pack[16:24]
     first, second = [None] * 8, [None] * 8
     third = None
@@ -299,6 +308,23 @@
         out[2 * s + 1, :, 1024:1152] = acc
 
 
+def expand(v, fout, obuf):
+    row, col = lanes((16, N))
+    repeat = marks(row == col % 16)
+    choose = sum_y()
+    row, col = lanes((512, N))
+    hi, lo = [
+        jnp.where(row % 8 == col // 16, mul(choose, mul(part, repeat, TN).astype(BF16)), 0.0).astype(BF16)
+        for part in split(fout[...])
+    ]
+    w = jnp.concatenate([hi, hi, lo], axis=1)
+    parts = jnp.concatenate([v[0:128], v[128:256], v[0:128]], axis=0)
+    for q in range(4):
+        u = mul(w[q * 128 : (q + 1) * 128], parts)
+        for x in range(8):
+            obuf[q * 16 : (q + 1) * 16, x] = u[:, x * N : (x + 1) * N].reshape(16, 8, N).astype(BF16)
+
+
 def core_tile(data, f3w, fact_in, get_sel, tsel):
     fact = data[0, :, 1024:1152]
     for d in range(1, 16):
@@ -319,46 +345,43 @@
 
 
 def space_kernel(
-    data, zf, f3w, fact_in, flow, cot, sel, out, vfirst, second, vsecond, tsel, sems
+    data, zf, f3w, fact_in, flow, fout, cot, sel, out, obuf, vout, second, tsel, sems
 ):
     sy = sum_y()
-    vout = (vfirst, vsecond)
-    get_sel = pltpu.make_async_copy(sel, tsel, sems.at[8])
+    get_sel = pltpu.make_async_copy(sel, tsel, sems.at[1])
     get_sel.start()
-    loads = []
-    for part in range(4):
-        rows = pl.ds(16 * part, 16)
-        load = pltpu.make_async_copy(cot.at[rows], second.at[rows], sems.at[part])
-        load.start()
-        loads.append(load)
-    zh, zl = zf[:128], zf[128:]
+    load = pltpu.make_async_copy(cot, second, sems.at[0])
+    load.start()
+    zl = zf[128:]
+    zz = jnp.concatenate([zf[:128], zf[:128]], axis=0)
     for g in range(4):
         v = data[:, :, g * 256 : (g + 1) * 256].reshape(128, 256)
         hi, lo = split(v)
-        r = mul(hi, zh, TN) + mul(lo, zh, TN) + mul(hi, zl, TN)
+        r = mul(jnp.concatenate([hi, lo], axis=0), zz, TN) + mul(hi, zl, TN)
         rh, rl = split(r)
         for x in range(8):
             for f in range(2):
                 for y2 in range(2):
                     row = (2 * g + y2) * 16
-                    src = slice(x * 32 + f * 16, x * 32 + f * 16 + 16)
+                    src = slice(f * 128 + x * 16, f * 128 + x * 16 + 16)
                     cols = slice(y2 * N, (y2 + 1) * N)
-                    vout[f][row : row + 16, x * N : (x + 1) * N] = rh[src, cols]
-                    vout[f][128 + row : 128 + row + 16, x * N : (x + 1) * N] = rl[src, cols]
+                    vout[f, row : row + 16, x * N : (x + 1) * N] = rh[src, cols]
+                    vout[f, 128 + row : 128 + row + 16, x * N : (x + 1) * N] = rl[src, cols]
     ri, ci = lanes((128, 512))
     same = ri // 16 == ci % 8
     res = []
     for f, field in enumerate((flow, second)):
-        for load in loads if f else ():
+        if f == 1:
             load.wait()
         u = jnp.concatenate([plane(field, x) for x in range(8)], axis=1)
-        part = mul(vout[1 - f][...], u, NT)
+        part = mul(vout[1 - f], u, NT)
         p = jnp.where(same, part[:128] + part[128:], 0.0)
         q = p[0:16]
         for yy in range(1, 8):
             q = q + p[yy * 16 : yy * 16 + 16]
         res.append(pick(q, sy))
         if f == 0:
+            expand(vout.at[0], fout, obuf)
             last = core_tile(data, f3w, fact_in, get_sel, tsel)
     both = jnp.concatenate(res, axis=1)
     row = jnp.concatenate([both[0:8], both[8:16], last], axis=1)
@@ -418,31 +441,9 @@
     return sends
 
 
-def expand(v, fout, field, obuf, sems):
-    row, col = lanes((16, N))
-    repeat = marks(row == col % 16)
-    choose = sum_y()
-    row, col = lanes((512, N))
-    hi, lo = [
-        jnp.where(row % 8 == col // 16, mul(choose, mul(part, repeat, TN).astype(BF16)), 0.0).astype(BF16)
-        for part in split(fout[...])
-    ]
-    w = jnp.concatenate([hi, hi, lo], axis=1)
-    parts = jnp.concatenate([v[0:128], v[128:256], v[0:128]], axis=0)
-    puts = []
-    for q in range(4):
-        u = mul(w[q * 128 : (q + 1) * 128], parts)
-        for x in range(8):
-            obuf[q * 16 : (q + 1) * 16, x] = u[:, x * N : (x + 1) * N].reshape(16, 8, N).astype(BF16)
-        put = pltpu.make_async_copy(
-            obuf.at[pl.ds(16 * q, 16)], field.at[pl.ds(16 * q, 16)], sems.at[2 + q]
-        )
-        put.start()
-        puts.append(put)
-    return puts
-
-
-def own_kernel(data, v, fout, sums, core, field, g1, g2, g3, mine, buf, obuf, gbuf, sems):
+def own_kernel(data, obuf, sums, core, field, g1, g2, g3, mine, buf, gbuf, sems):
+    put = pltpu.make_async_copy(obuf, field, sems.at[2])
+    put.start()
     sends = write_half(data, core, buf, sems, lax.axis_index("py") % 2)
     total = data[0, :, 0:N]
     for d in range(1, 16):
@@ -457,11 +458,10 @@
     gbuf[1] = sums[:, 32:64]
     gbuf[2] = third[:, :32]
     for i, dst in enumerate((g1, g2, g3)):
-        send = pltpu.make_async_copy(gbuf.at[i], dst, sems.at[6 + i])
+        send = pltpu.make_async_copy(gbuf.at[i], dst, sems.at[3 + i])
         send.start()
         sends.append(send)
-    sends += expand(v, fout, field, obuf, sems)
-    for send in sends:
+    for send in sends + [put]:
         send.wait()
 
 
@@ -561,17 +561,17 @@
         r3, yf, f2w, gk, flat, pack
     )
     r4 = exchange(o4, "py")
-    o5, v = call(
+    o5, obuf = call(
         space_kernel,
-        (5, 2),
-        [((16, 8, 384), F32), ((256, 1024), BF16)],
+        (6, 2),
+        [((16, 8, 384), F32), ((64, 8, 8, N), BF16)],
         [
+            pltpu.VMEM((2, 256, 1024), BF16),
             pltpu.VMEM((64, 8, 8, N), BF16),
-            pltpu.VMEM((256, 1024), BF16),
             pltpu.VMEM((1024, N), BF16),
-            DMA((9,)),
+            DMA((2,)),
         ],
-    )(r4, tab["zf"], f3w, fact, flow, cot, tab["sel"])
+    )(r4, tab["zf"], f3w, fact, flow, fout, cot, tab["sel"])
     r5 = exchange(o5, "px")
     o6, sums = call(gather_kernel, (1, 0), [((16, 8, 768), F32), ((8, N), F32)])(r5)
     r6 = exchange(o6, "py")
@@ -581,11 +581,11 @@
     small = ((8, 32), F32, HB)
     gcore, field, g1, g2, g3, mine = call(
         own_kernel,
-        (4, 0),
+        (3, 0),
         [whole, ((64, 8, 8, N), BF16, HB), small, small, small, ((8, N), F32)],
-        [half, pltpu.VMEM((64, 8, 8, N), BF16), pltpu.VMEM((3, 8, 32), F32), DMA((9,))],
+        [half, pltpu.VMEM((3, 8, 32), F32), DMA((6,))],
         flops=100_000_000,
-    )(r6, v, fout, sums)
+    )(r6, obuf, sums)
     small = ((16, 64), F32, HB)
     gcore, gin, gout = call(
         other_kernel,

time: 110 us -> 109 us (level)
  no operation moved by 1% of the time
where the time goes in v4:
time: 109 us; the launch traced here: 108 us
  blocking collectives  74.5 us (68%)
  Pallas kernels  15.3 us (14%)
  starting transfers between devices  11.3 us (10%)
  waiting for transfers between devices  6.51 us (6%)
    all_to_all x5, blocking collectives, exchange(): return lax.all_to_all(v, axis, split_axis=0, concat_axis=0, tiled=True)  74.5 us
    pallas_call x9, Pallas kernels, placed(): return run(*args[:ins[0]], *far)  15.3 us
    all_to_all x1, starting transfers between devices, exchange(): return lax.all_to_all(v, axis, split_axis=0, concat_axis=0, tiled=True)  10.6 us
    all_to_all x1, waiting for transfers between devices, exchange(): return lax.all_to_all(v, axis, split_axis=0, concat_axis=0, tiled=True)  6.51 us
  transfers between devices with their start and end apart: 2, of which 1 were waited for; matrix products, arithmetic and copies ran while one was open for 0% of the time, Pallas kernels for 5%

profile of v4, /device:TPU:1, one launch (start us, length us, event | category | flops | bytes accessed | tf_op | source)
XLA Modules:
  0.0 108.3 jit_solution(8197700815179889006)
XLA Ops:
  0.6 2.8 %shard_map.171 = (f32[16,8,1024]{2,1,0:T(8,128)S(1)}, bf16[256,512]{1,0:T(8,128)(2,1)S(1)}, f32[16,64]{1,0:T(8,128)S(1)}) custom-call(bf16[64,8,8,128]{3,2,1,0:T(8,128)(2,1)} %flow.3, bf16[64,8,8,128]{3,2,1,0:T(8,128)(2,1)} %cot.3, f32[16,64]{1,0:T(8,128)} %bitcast.16, f32[16,64]{1,0:T(8,128)} %bitcast.17, bf16[256,256]{1,0:T(8,128)(2,1)} %constant.8.clone.zf, ...), custom_call_target="tpu_custom_call" | custom-call | flops 1000000 | bytes 1000000 | tf_op jit(solution)/shard_map/pallas_call | solution.py:510
  3.4 16.3 %all_to_all.30.data = f32[16,8,1024]{2,1,0:T(8,128)S(1)} all-to-all(f32[16,8,1024]{2,1,0:T(8,128)S(1)} %get-tuple-element.39), channel_id=1, replica_groups=mesh['px'=16,'py'=16] {'py'}, dimensions={0} | all-to-all | bytes 1048576 | tf_op jit(solution)/shard_map/all_to_all | solution.py:516
  19.7 0.9 shard_map.172
  20.7 10.6 %all-to-all-start.1 = ((f32[16,8,256]{2,1,0:T(8,128)}), f32[16,8,256]{2,1,0:T(8,128)S(1)}, u32[]{:S(2)}, u32[]{:S(2)}) async-start(f32[16,8,256]{2,1,0:T(8,128)} %shard_map.172), calls=%async_computation.1 | async-start | bytes 262144 | tf_op jit(solution)/shard_map/all_to_all | solution.py:516
  31.3 0.0 copy-start
  31.3 0.0 copy-start.1
  31.3 3.4 %shard_map.173 = (f32[256,128]{1,0:T(8,128)S(1)}, f32[256,512]{1,0:T(8,128)S(1)}, bf16[2,1024,256]{2,1,0:T(8,128)(2,1)S(1)}, f32[32,128]{1,0:T(8,128)S(1)}, f32[...) custom-call(f32[8,32]{1,0:T(8,128)} %bitcast.18, f32[8,32]{1,0:T(8,128)} %bitcast.19, ...), custom_call_target="tpu_custom_call" | custom-call | flops 100000000 | bytes 1000000 | tf_op jit(solution)/shard_map/pallas_call | solution.py:510
  34.8 6.5 %all-to-all-done.1.data = f32[16,8,256]{2,1,0:T(8,128)S(1)} async-done(((f32[16,8,256]{2,1,0:T(8,128)}), f32[16,8,256]{2,1,0:T(8,128)S(1)}, u32[]{:S(2)}, u32[]{:S(2)}) %all-to-all-start.1) | async-done | bytes 131104 | tf_op jit(solution)/shard_map/all_to_all | solution.py:516
  41.3 1.1 %shard_map.174 = (f32[16,8,384]{2,1,0:T(8,128)S(1)}, f32[256,128]{1,0:T(8,128)S(1)}) custom-call(f32[16,8,256]{2,1,0:T(8,128)S(1)} %all-to-all-done.1.data, f32[256,128]{1,0:T(8,128)S(1)} %get-tuple-element.46.kern, f32[32,128]{1,0:T(8,128)S(1)} %get-tuple-element.47.pack, f32[128,128]{1,0:T(8,128)S(1)} %get-tuple-element.48.ex, ...), custom_call_target="tpu_custom_call" | custom-call | flops 1000000 | bytes 1000000 | tf_op jit(solution)/shard_map/pallas_call | solution.py:510
  42.4 13.4 %all_to_all.31.data = f32[16,8,384]{2,1,0:T(8,128)S(1)} all-to-all(f32[16,8,384]{2,1,0:T(8,128)S(1)} %get-tuple-element.50), channel_id=1, replica_groups=mesh['px'=16,'py'=16] {'px'}, dimensions={0} | all-to-all | bytes 393216 | tf_op jit(solution)/shard_map/all_to_all | solution.py:516
  55.8 0.7 shard_map.175
  56.5 17.5 %all_to_all.32.data = f32[16,8,1152]{2,1,0:T(8,128)S(1)} all-to-all(f32[16,8,1152]{2,1,0:T(8,128)S(1)} %get-tuple-element.54), channel_id=1, replica_groups=mesh['px'=16,'py'=16] {'py'}, dimensions={0} | all-to-all | bytes 1179648 | tf_op jit(solution)/shard_map/all_to_all | solution.py:516
  74.0 0.0 copy-done
  74.0 0.0 copy-done.1
  74.0 2.8 %shard_map.176 = (f32[16,8,384]{2,1,0:T(8,128)S(1)}, bf16[64,8,8,128]{3,2,1,0:T(8,128)(2,1)S(1)}) custom-call(f32[16,8,1152]{2,1,0:T(8,128)S(1)} %all_to_all.32.data, bf16[256,256]{1,0:T(8,128)(2,1)S(1)} %copy-done.1, f32[128,128]{1,0:T(8,128)S(1)} %get-tuple-element.55.f3w, f32[8,128]{1,0:T(8,128)S(1)} %get-tuple-element.56.fact_in, ...), custom_call_target="tpu_custom_call" | custom-call | flops 1000000 | bytes 1000000 | tf_op jit(solution)/shard_map/pallas_call | solution.py:510
  76.8 14.0 %all_to_all.33.data = f32[16,8,384]{2,1,0:T(8,128)S(1)} all-to-all(f32[16,8,384]{2,1,0:T(8,128)S(1)} %get-tuple-element.58), channel_id=1, replica_groups=mesh['px'=16,'py'=16] {'px'}, dimensions={0} | all-to-all | bytes 393216 | tf_op jit(solution)/shard_map/all_to_all | solution.py:516
  90.9 0.1 shard_map.177
  91.0 13.2 %all_to_all.34.data = f32[16,8,768]{2,1,0:T(8,128)S(1)} all-to-all(f32[16,8,768]{2,1,0:T(8,128)S(1)} %get-tuple-element.59), channel_id=1, replica_groups=mesh['px'=16,'py'=16] {'py'}, dimensions={0} | all-to-all | bytes 786432 | tf_op jit(solution)/shard_map/all_to_all | solution.py:516
  104.2 0.6 collective-permute-start
  104.9 1.7 %shard_map.178 = (f32[16,8,8,8,16]{4,3,2,1,0:T(8,128)}, bf16[64,8,8,128]{3,2,1,0:T(8,128)(2,1)}, f32[8,32]{1,0:T(8,128)}, f32[8,32]{1,0:T(8,128)}, f32[8,32]{1,0:T(8,128)}, /*index=5*/f32[8,128]{1,0:T(8,128)S(1)}) custom-call(f32[16,8,768]{2,1,0:T(8,128)S(1)} %all_to_all.34.data, bf16[64,8,8,128]{3,2,1,0:T(8,128)(2,1)S(1)} %get-tuple-element.60.obuf, ...), custom_call_target="tpu_custom_call" | custom-call | flops 100000000 | bytes 1000000 | tf_op jit(solution)/shard_map/pallas_call | solution.py:510
  106.6 0.0 collective-permute-done.data
  106.6 1.7 %shard_map.179 = (f32[16,8,8,8,16]{4,3,2,1,0:T(8,128)}, f32[16,64]{1,0:T(8,128)}, f32[16,64]{1,0:T(8,128)}) custom-call(f32[16,8,768]{2,1,0:T(8,128)S(1)} %collective-permute-done.data, f32[8,128]{1,0:T(8,128)S(1)} %get-tuple-element.63.mine, f32[16,8,8,8,16]{4,3,2,1,0:T(8,128)} %get-tuple-element.64.core_in), custom_call_target="tpu_custom_call", output_to_operand_aliasing={{0}: (2, {})} | custom-call | flops 1000000 | bytes 1000000 | tf_op jit(solution)/shard_map/pallas_call | solution.py:510
Async XLA Ops:
  20.7 20.6 %all-to-all-start.1 = ((f32[16,8,256]{2,1,0:T(8,128)}), f32[16,8,256]{2,1,0:T(8,128)S(1)}, u32[]{:S(2)}, u32[]{:S(2)}) async-start(f32[16,8,256]{2,1,0:T(8,128)} %shard_map.172), calls=%async_computation.1 | async-start | bytes 262144 | tf_op jit(solution)/shard_map/all_to_all | solution.py:516
  31.3 42.7 %copy-start = (bf16[64,8,8,128]{3,2,1,0:T(8,128)(2,1)S(1)}, bf16[64,8,8,128]{3,2,1,0:T(8,128)(2,1)}, u32[]{:S(2)}) copy-start(bf16[64,8,8,128]{3,2,1,0:T(8,128)(2,1)} %flow.3) | copy-start | bytes 3145732
  31.3 42.7 %copy-start.1 = (bf16[256,256]{1,0:T(8,128)(2,1)S(1)}, bf16[256,256]{1,0:T(8,128)(2,1)}, u32[]{:S(2)}) copy-start(bf16[256,256]{1,0:T(8,128)(2,1)} %constant.8.clone.zf) | copy-start | bytes 393220
  104.2 2.4 %collective-permute-start = (f32[16,8,768]{2,1,0:T(8,128)S(1)}, f32[16,8,768]{2,1,0:T(8,128)S(1)}, u32[]{:S(2)}, u32[]{:S(2)}) collective-permute-start(f32[16,8,768]{2,1,0:T(8,128)S(1)} %all_to_all.34.data), channel_id=1, source_target_pairs={{0,1},{1,0},{2,3},{3,2},{4,5},{5,4},{6,7},{7,6},{8,9},{9,8},{10,11... | collective-permute-start | bytes 1179656 | tf_op jit(solution)/shard_map/ppermute | solution.py:578

commit v5 on v4

--- a/solution.py
+++ b/solution.py
@@ -139,8 +139,8 @@
     for copy in small:
         copy.wait()
     sy = sum_y()
-    for f, factor in enumerate((tin, tout)):
-        w = jnp.concatenate(spread(factor[...], sy), axis=0)
+    weights = [jnp.concatenate(spread(factor[...], sy), axis=0) for factor in (tin, tout)]
+    for f, w in enumerate(weights):
         large[f].wait()
         for pair in range(4):
             u = jnp.concatenate(
@@ -214,8 +214,7 @@
     for a in range(16):
         loads[a].wait()
         flat[a * 16 : (a + 1) * 16, :] = cbuf[a].T
-    ch, cl = split(flat[...])
-    kern[...] = mul(ch, wh) + mul(cl, wh) + mul(ch, wl)
+    kern[...] = stacked(flat[...], wh, wl)
     get.wait()
 
 
@@ -348,10 +347,14 @@
     data, zf, f3w, fact_in, flow, fout, cot, sel, out, obuf, vout, second, tsel, sems
 ):
     sy = sum_y()
+    loads = [
+        pltpu.make_async_copy(cot.at[pl.ds(16 * i, 16)], second.at[pl.ds(16 * i, 16)], sems.at[2 + i])
+        for i in range(4)
+    ]
+    for load in loads:
+        load.start()
     get_sel = pltpu.make_async_copy(sel, tsel, sems.at[1])
     get_sel.start()
-    load = pltpu.make_async_copy(cot, second, sems.at[0])
-    load.start()
     zl = zf[128:]
     zz = jnp.concatenate([zf[:128], zf[:128]], axis=0)
     for g in range(4):
@@ -371,7 +374,7 @@
     same = ri // 16 == ci % 8
     res = []
     for f, field in enumerate((flow, second)):
-        if f == 1:
+        for load in loads if f else ():
             load.wait()
         u = jnp.concatenate([plane(field, x) for x in range(8)], axis=1)
         part = mul(vout[1 - f], u, NT)
@@ -382,7 +385,7 @@
         res.append(pick(q, sy))
         if f == 0:
             expand(vout.at[0], fout, obuf)
-            last = core_tile(data, f3w, fact_in, get_sel, tsel)
+    last = core_tile(data, f3w, fact_in, get_sel, tsel)
     both = jnp.concatenate(res, axis=1)
     row = jnp.concatenate([both[0:8], both[8:16], last], axis=1)
     for d in range(16):
@@ -569,7 +572,7 @@
             pltpu.VMEM((2, 256, 1024), BF16),
             pltpu.VMEM((64, 8, 8, N), BF16),
             pltpu.VMEM((1024, N), BF16),
-            DMA((2,)),
+            DMA((6,)),
         ],
     )(r4, tab["zf"], f3w, fact, flow, fout, cot, tab["sel"])
     r5 = exchange(o5, "px")

time: 109 us -> 109 us (level)
  no operation moved by 1% of the time
where the time goes in v5:
time: 109 us; the launch traced here: 108 us
  blocking collectives  74.5 us (68%)
  Pallas kernels  15.3 us (14%)
  starting transfers between devices  11.3 us (10%)
  waiting for transfers between devices  6.51 us (6%)
    all_to_all x5, blocking collectives, exchange(): return lax.all_to_all(v, axis, split_axis=0, concat_axis=0, tiled=True)  74.5 us
    pallas_call x9, Pallas kernels, placed(): return run(*args[:ins[0]], *far)  15.3 us
    all_to_all x1, starting transfers between devices, exchange(): return lax.all_to_all(v, axis, split_axis=0, concat_axis=0, tiled=True)  10.6 us
    all_to_all x1, waiting for transfers between devices, exchange(): return lax.all_to_all(v, axis, split_axis=0, concat_axis=0, tiled=True)  6.51 us
  transfers between devices with their start and end apart: 2, of which 1 were waited for; matrix products, arithmetic and copies ran while one was open for 0% of the time, Pallas kernels for 5%

profile of v5, /device:TPU:1, one launch (start us, length us, event | category | flops | bytes accessed | tf_op | source)
XLA Modules:
  0.0 108.3 jit_solution(775458576367905388)
XLA Ops:
  0.6 2.7 %shard_map.171 = (f32[16,8,1024]{2,1,0:T(8,128)S(1)}, bf16[256,512]{1,0:T(8,128)(2,1)S(1)}, f32[16,64]{1,0:T(8,128)S(1)}) custom-call(bf16[64,8,8,128]{3,2,1,0:T(8,128)(2,1)} %flow.3, bf16[64,8,8,128]{3,2,1,0:T(8,128)(2,1)} %cot.3, f32[16,64]{1,0:T(8,128)} %bitcast.16, f32[16,64]{1,0:T(8,128)} %bitcast.17, bf16[256,256]{1,0:T(8,128)(2,1)} %constant.8.clone.zf, ...), custom_call_target="tpu_custom_call" | custom-call | flops 1000000 | bytes 1000000 | tf_op jit(solution)/shard_map/pallas_call | solution.py:513
  3.4 16.3 %all_to_all.30.data = f32[16,8,1024]{2,1,0:T(8,128)S(1)} all-to-all(f32[16,8,1024]{2,1,0:T(8,128)S(1)} %get-tuple-element.39), channel_id=1, replica_groups=mesh['px'=16,'py'=16] {'py'}, dimensions={0} | all-to-all | bytes 1048576 | tf_op jit(solution)/shard_map/all_to_all | solution.py:519
  19.7 0.9 shard_map.172
  20.6 10.6 %all-to-all-start.1 = ((f32[16,8,256]{2,1,0:T(8,128)}), f32[16,8,256]{2,1,0:T(8,128)S(1)}, u32[]{:S(2)}, u32[]{:S(2)}) async-start(f32[16,8,256]{2,1,0:T(8,128)} %shard_map.172), calls=%async_computation.1 | async-start | bytes 262144 | tf_op jit(solution)/shard_map/all_to_all | solution.py:519
  31.3 0.0 copy-start
  31.3 0.0 copy-start.1
  31.3 3.4 %shard_map.173 = (f32[256,128]{1,0:T(8,128)S(1)}, f32[256,512]{1,0:T(8,128)S(1)}, bf16[2,1024,256]{2,1,0:T(8,128)(2,1)S(1)}, f32[32,128]{1,0:T(8,128)S(1)}, f32[...) custom-call(f32[8,32]{1,0:T(8,128)} %bitcast.18, f32[8,32]{1,0:T(8,128)} %bitcast.19, ...), custom_call_target="tpu_custom_call" | custom-call | flops 100000000 | bytes 1000000 | tf_op jit(solution)/shard_map/pallas_call | solution.py:513
  34.7 6.5 %all-to-all-done.1.data = f32[16,8,256]{2,1,0:T(8,128)S(1)} async-done(((f32[16,8,256]{2,1,0:T(8,128)}), f32[16,8,256]{2,1,0:T(8,128)S(1)}, u32[]{:S(2)}, u32[]{:S(2)}) %all-to-all-start.1) | async-done | bytes 131104 | tf_op jit(solution)/shard_map/all_to_all | solution.py:519
  41.2 1.1 %shard_map.174 = (f32[16,8,384]{2,1,0:T(8,128)S(1)}, f32[256,128]{1,0:T(8,128)S(1)}) custom-call(f32[16,8,256]{2,1,0:T(8,128)S(1)} %all-to-all-done.1.data, f32[256,128]{1,0:T(8,128)S(1)} %get-tuple-element.46.kern, f32[32,128]{1,0:T(8,128)S(1)} %get-tuple-element.47.pack, f32[128,128]{1,0:T(8,128)S(1)} %get-tuple-element.48.ex, ...), custom_call_target="tpu_custom_call" | custom-call | flops 1000000 | bytes 1000000 | tf_op jit(solution)/shard_map/pallas_call | solution.py:513
  42.3 13.4 %all_to_all.31.data = f32[16,8,384]{2,1,0:T(8,128)S(1)} all-to-all(f32[16,8,384]{2,1,0:T(8,128)S(1)} %get-tuple-element.50), channel_id=1, replica_groups=mesh['px'=16,'py'=16] {'px'}, dimensions={0} | all-to-all | bytes 393216 | tf_op jit(solution)/shard_map/all_to_all | solution.py:519
  55.7 0.7 shard_map.175
  56.4 17.5 %all_to_all.32.data = f32[16,8,1152]{2,1,0:T(8,128)S(1)} all-to-all(f32[16,8,1152]{2,1,0:T(8,128)S(1)} %get-tuple-element.54), channel_id=1, replica_groups=mesh['px'=16,'py'=16] {'py'}, dimensions={0} | all-to-all | bytes 1179648 | tf_op jit(solution)/shard_map/all_to_all | solution.py:519
  74.0 0.0 copy-done
  74.0 0.0 copy-done.1
  74.0 2.9 %shard_map.176 = (f32[16,8,384]{2,1,0:T(8,128)S(1)}, bf16[64,8,8,128]{3,2,1,0:T(8,128)(2,1)S(1)}) custom-call(f32[16,8,1152]{2,1,0:T(8,128)S(1)} %all_to_all.32.data, bf16[256,256]{1,0:T(8,128)(2,1)S(1)} %copy-done.1, f32[128,128]{1,0:T(8,128)S(1)} %get-tuple-element.55.f3w, f32[8,128]{1,0:T(8,128)S(1)} %get-tuple-element.56.fact_in, ...), custom_call_target="tpu_custom_call" | custom-call | flops 1000000 | bytes 1000000 | tf_op jit(solution)/shard_map/pallas_call | solution.py:513
  76.8 14.0 %all_to_all.33.data = f32[16,8,384]{2,1,0:T(8,128)S(1)} all-to-all(f32[16,8,384]{2,1,0:T(8,128)S(1)} %get-tuple-element.58), channel_id=1, replica_groups=mesh['px'=16,'py'=16] {'px'}, dimensions={0} | all-to-all | bytes 393216 | tf_op jit(solution)/shard_map/all_to_all | solution.py:519
  90.8 0.1 shard_map.177
  91.0 13.2 %all_to_all.34.data = f32[16,8,768]{2,1,0:T(8,128)S(1)} all-to-all(f32[16,8,768]{2,1,0:T(8,128)S(1)} %get-tuple-element.59), channel_id=1, replica_groups=mesh['px'=16,'py'=16] {'py'}, dimensions={0} | all-to-all | bytes 786432 | tf_op jit(solution)/shard_map/all_to_all | solution.py:519
  104.2 0.6 collective-permute-start
  104.8 1.7 %shard_map.178 = (f32[16,8,8,8,16]{4,3,2,1,0:T(8,128)}, bf16[64,8,8,128]{3,2,1,0:T(8,128)(2,1)}, f32[8,32]{1,0:T(8,128)}, f32[8,32]{1,0:T(8,128)}, f32[8,32]{1,0:T(8,128)}, /*index=5*/f32[8,128]{1,0:T(8,128)S(1)}) custom-call(f32[16,8,768]{2,1,0:T(8,128)S(1)} %all_to_all.34.data, bf16[64,8,8,128]{3,2,1,0:T(8,128)(2,1)S(1)} %get-tuple-element.60.obuf, ...), custom_call_target="tpu_custom_call" | custom-call | flops 100000000 | bytes 1000000 | tf_op jit(solution)/shard_map/pallas_call | solution.py:513
  106.6 0.0 collective-permute-done.data
  106.6 1.7 %shard_map.179 = (f32[16,8,8,8,16]{4,3,2,1,0:T(8,128)}, f32[16,64]{1,0:T(8,128)}, f32[16,64]{1,0:T(8,128)}) custom-call(f32[16,8,768]{2,1,0:T(8,128)S(1)} %collective-permute-done.data, f32[8,128]{1,0:T(8,128)S(1)} %get-tuple-element.63.mine, f32[16,8,8,8,16]{4,3,2,1,0:T(8,128)} %get-tuple-element.64.core_in), custom_call_target="tpu_custom_call", output_to_operand_aliasing={{0}: (2, {})} | custom-call | flops 1000000 | bytes 1000000 | tf_op jit(solution)/shard_map/pallas_call | solution.py:513
Async XLA Ops:
  20.6 20.6 %all-to-all-start.1 = ((f32[16,8,256]{2,1,0:T(8,128)}), f32[16,8,256]{2,1,0:T(8,128)S(1)}, u32[]{:S(2)}, u32[]{:S(2)}) async-start(f32[16,8,256]{2,1,0:T(8,128)} %shard_map.172), calls=%async_computation.1 | async-start | bytes 262144 | tf_op jit(solution)/shard_map/all_to_all | solution.py:519
  31.3 42.7 %copy-start = (bf16[64,8,8,128]{3,2,1,0:T(8,128)(2,1)S(1)}, bf16[64,8,8,128]{3,2,1,0:T(8,128)(2,1)}, u32[]{:S(2)}) copy-start(bf16[64,8,8,128]{3,2,1,0:T(8,128)(2,1)} %flow.3) | copy-start | bytes 3145732
  31.3 42.7 %copy-start.1 = (bf16[256,256]{1,0:T(8,128)(2,1)S(1)}, bf16[256,256]{1,0:T(8,128)(2,1)}, u32[]{:S(2)}) copy-start(bf16[256,256]{1,0:T(8,128)(2,1)} %constant.8.clone.zf) | copy-start | bytes 393220
  104.2 2.4 %collective-permute-start = (f32[16,8,768]{2,1,0:T(8,128)S(1)}, f32[16,8,768]{2,1,0:T(8,128)S(1)}, u32[]{:S(2)}, u32[]{:S(2)}) collective-permute-start(f32[16,8,768]{2,1,0:T(8,128)S(1)} %all_to_all.34.data), channel_id=1, source_target_pairs={{0,1},{1,0},{2,3},{3,2},{4,5},{5,4},{6,7},{7,6},{8,9},{9,8},{10,11... | collective-permute-start | bytes 1179656 | tf_op jit(solution)/shard_map/ppermute | solution.py:581

commit v6 on v5

--- a/solution.py
+++ b/solution.py
@@ -203,13 +203,15 @@
     w = jnp.concatenate(
         [f1[r : r + 1] * f2[s : s + 1] * f3 for r in range(8) for s in range(8)], axis=0
     )
-    row, col = lanes((32, 16 * N))
-    block, lane = col // N, col % N
-    wide2 = pick(f2t[...], marks(row == 2 * block + lane // 16 % 2))
-    wide3 = pick(f3t[...], marks((row == 2 * block + lane // 8 % 2) & (lane < 32)))
-    for d in range(16):
-        f2w[d * 8 : d * 8 + 8] = wide2[:, d * N : (d + 1) * N]
-        f3w[d * 8 : d * 8 + 8] = wide3[:, d * N : (d + 1) * N]
+    row, lane = lanes((N, N))
+    zero = jnp.zeros((8, 96), F32)
+    for src, dst, where in (
+        (f2t, f2w, row == lane // 16 % 2),
+        (f3t, f3w, (row == lane // 8 % 2) & (lane < 32)),
+    ):
+        wide = jnp.concatenate([src[...], zero], axis=1)
+        moved = [wide] + [pltpu.roll(wide, N - 2 * d, 1) for d in range(1, 16)]
+        dst[...] = pick(jnp.concatenate(moved, axis=0), marks(where))
     wh, wl = split(w)
     for a in range(16):
         loads[a].wait()

time: 109 us -> 109 us (level)
  no operation moved by 1% of the time
where the time goes in v6:
time: 109 us; the launch traced here: 108 us
  blocking collectives  74.5 us (68%)
  Pallas kernels  15.3 us (14%)
  starting transfers between devices  11.3 us (10%)
  waiting for transfers between devices  6.56 us (6%)
    all_to_all x5, blocking collectives, exchange(): return lax.all_to_all(v, axis, split_axis=0, concat_axis=0, tiled=True)  74.5 us
    pallas_call x9, Pallas kernels, placed(): return run(*args[:ins[0]], *far)  15.3 us
    all_to_all x1, starting transfers between devices, exchange(): return lax.all_to_all(v, axis, split_axis=0, concat_axis=0, tiled=True)  10.6 us
    all_to_all x1, waiting for transfers between devices, exchange(): return lax.all_to_all(v, axis, split_axis=0, concat_axis=0, tiled=True)  6.56 us
  transfers between devices with their start and end apart: 2, of which 1 were waited for; matrix products, arithmetic and copies ran while one was open for 0% of the time, Pallas kernels for 5%

profile of v6, /device:TPU:1, one launch (start us, length us, event | category | flops | bytes accessed | tf_op | source)
XLA Modules:
  0.0 108.3 jit_solution(407720807742950280)
XLA Ops:
  0.6 2.7 %shard_map.171 = (f32[16,8,1024]{2,1,0:T(8,128)S(1)}, bf16[256,512]{1,0:T(8,128)(2,1)S(1)}, f32[16,64]{1,0:T(8,128)S(1)}) custom-call(bf16[64,8,8,128]{3,2,1,0:T(8,128)(2,1)} %flow.3, bf16[64,8,8,128]{3,2,1,0:T(8,128)(2,1)} %cot.3, f32[16,64]{1,0:T(8,128)} %bitcast.16, f32[16,64]{1,0:T(8,128)} %bitcast.17, bf16[256,256]{1,0:T(8,128)(2,1)} %constant.8.clone.zf, ...), custom_call_target="tpu_custom_call" | custom-call | flops 1000000 | bytes 1000000 | tf_op jit(solution)/shard_map/pallas_call | solution.py:515
  3.4 16.3 %all_to_all.30.data = f32[16,8,1024]{2,1,0:T(8,128)S(1)} all-to-all(f32[16,8,1024]{2,1,0:T(8,128)S(1)} %get-tuple-element.39), channel_id=1, replica_groups=mesh['px'=16,'py'=16] {'py'}, dimensions={0} | all-to-all | bytes 1048576 | tf_op jit(solution)/shard_map/all_to_all | solution.py:521
  19.7 0.9 shard_map.172
  20.6 10.6 %all-to-all-start.1 = ((f32[16,8,256]{2,1,0:T(8,128)}), f32[16,8,256]{2,1,0:T(8,128)S(1)}, u32[]{:S(2)}, u32[]{:S(2)}) async-start(f32[16,8,256]{2,1,0:T(8,128)} %shard_map.172), calls=%async_computation.1 | async-start | bytes 262144 | tf_op jit(solution)/shard_map/all_to_all | solution.py:521
  31.3 0.0 copy-start
  31.3 0.0 copy-start.1
  31.3 3.4 %shard_map.173 = (f32[256,128]{1,0:T(8,128)S(1)}, f32[256,512]{1,0:T(8,128)S(1)}, bf16[2,1024,256]{2,1,0:T(8,128)(2,1)S(1)}, f32[32,128]{1,0:T(8,128)S(1)}, f32[...) custom-call(f32[8,32]{1,0:T(8,128)} %bitcast.18, f32[8,32]{1,0:T(8,128)} %bitcast.19, ...), custom_call_target="tpu_custom_call" | custom-call | flops 100000000 | bytes 1000000 | tf_op jit(solution)/shard_map/pallas_call | solution.py:515
  34.7 6.6 %all-to-all-done.1.data = f32[16,8,256]{2,1,0:T(8,128)S(1)} async-done(((f32[16,8,256]{2,1,0:T(8,128)}), f32[16,8,256]{2,1,0:T(8,128)S(1)}, u32[]{:S(2)}, u32[]{:S(2)}) %all-to-all-start.1) | async-done | bytes 131104 | tf_op jit(solution)/shard_map/all_to_all | solution.py:521
  41.2 1.1 %shard_map.174 = (f32[16,8,384]{2,1,0:T(8,128)S(1)}, f32[256,128]{1,0:T(8,128)S(1)}) custom-call(f32[16,8,256]{2,1,0:T(8,128)S(1)} %all-to-all-done.1.data, f32[256,128]{1,0:T(8,128)S(1)} %get-tuple-element.46.kern, f32[32,128]{1,0:T(8,128)S(1)} %get-tuple-element.47.pack, f32[128,128]{1,0:T(8,128)S(1)} %get-tuple-element.48.ex, ...), custom_call_target="tpu_custom_call" | custom-call | flops 1000000 | bytes 1000000 | tf_op jit(solution)/shard_map/pallas_call | solution.py:515
  42.3 13.4 %all_to_all.31.data = f32[16,8,384]{2,1,0:T(8,128)S(1)} all-to-all(f32[16,8,384]{2,1,0:T(8,128)S(1)} %get-tuple-element.50), channel_id=1, replica_groups=mesh['px'=16,'py'=16] {'px'}, dimensions={0} | all-to-all | bytes 393216 | tf_op jit(solution)/shard_map/all_to_all | solution.py:521
  55.7 0.7 shard_map.175
  56.4 17.5 %all_to_all.32.data = f32[16,8,1152]{2,1,0:T(8,128)S(1)} all-to-all(f32[16,8,1152]{2,1,0:T(8,128)S(1)} %get-tuple-element.54), channel_id=1, replica_groups=mesh['px'=16,'py'=16] {'py'}, dimensions={0} | all-to-all | bytes 1179648 | tf_op jit(solution)/shard_map/all_to_all | solution.py:521
  74.0 0.0 copy-done
  74.0 0.0 copy-done.1
  74.0 2.9 %shard_map.176 = (f32[16,8,384]{2,1,0:T(8,128)S(1)}, bf16[64,8,8,128]{3,2,1,0:T(8,128)(2,1)S(1)}) custom-call(f32[16,8,1152]{2,1,0:T(8,128)S(1)} %all_to_all.32.data, bf16[256,256]{1,0:T(8,128)(2,1)S(1)} %copy-done.1, f32[128,128]{1,0:T(8,128)S(1)} %get-tuple-element.55.f3w, f32[8,128]{1,0:T(8,128)S(1)} %get-tuple-element.56.fact_in, ...), custom_call_target="tpu_custom_call" | custom-call | flops 1000000 | bytes 1000000 | tf_op jit(solution)/shard_map/pallas_call | solution.py:515
  76.8 14.0 %all_to_all.33.data = f32[16,8,384]{2,1,0:T(8,128)S(1)} all-to-all(f32[16,8,384]{2,1,0:T(8,128)S(1)} %get-tuple-element.58), channel_id=1, replica_groups=mesh['px'=16,'py'=16] {'px'}, dimensions={0} | all-to-all | bytes 393216 | tf_op jit(solution)/shard_map/all_to_all | solution.py:521
  90.8 0.1 shard_map.177
  91.0 13.2 %all_to_all.34.data = f32[16,8,768]{2,1,0:T(8,128)S(1)} all-to-all(f32[16,8,768]{2,1,0:T(8,128)S(1)} %get-tuple-element.59), channel_id=1, replica_groups=mesh['px'=16,'py'=16] {'py'}, dimensions={0} | all-to-all | bytes 786432 | tf_op jit(solution)/shard_map/all_to_all | solution.py:521
  104.2 0.6 collective-permute-start
  104.8 1.7 %shard_map.178 = (f32[16,8,8,8,16]{4,3,2,1,0:T(8,128)}, bf16[64,8,8,128]{3,2,1,0:T(8,128)(2,1)}, f32[8,32]{1,0:T(8,128)}, f32[8,32]{1,0:T(8,128)}, f32[8,32]{1,0:T(8,128)}, /*index=5*/f32[8,128]{1,0:T(8,128)S(1)}) custom-call(f32[16,8,768]{2,1,0:T(8,128)S(1)} %all_to_all.34.data, bf16[64,8,8,128]{3,2,1,0:T(8,128)(2,1)S(1)} %get-tuple-element.60.obuf, ...), custom_call_target="tpu_custom_call" | custom-call | flops 100000000 | bytes 1000000 | tf_op jit(solution)/shard_map/pallas_call | solution.py:515
  106.6 0.0 collective-permute-done.data
  106.6 1.7 %shard_map.179 = (f32[16,8,8,8,16]{4,3,2,1,0:T(8,128)}, f32[16,64]{1,0:T(8,128)}, f32[16,64]{1,0:T(8,128)}) custom-call(f32[16,8,768]{2,1,0:T(8,128)S(1)} %collective-permute-done.data, f32[8,128]{1,0:T(8,128)S(1)} %get-tuple-element.63.mine, f32[16,8,8,8,16]{4,3,2,1,0:T(8,128)} %get-tuple-element.64.core_in), custom_call_target="tpu_custom_call", output_to_operand_aliasing={{0}: (2, {})} | custom-call | flops 1000000 | bytes 1000000 | tf_op jit(solution)/shard_map/pallas_call | solution.py:515
Async XLA Ops:
  20.6 20.6 %all-to-all-start.1 = ((f32[16,8,256]{2,1,0:T(8,128)}), f32[16,8,256]{2,1,0:T(8,128)S(1)}, u32[]{:S(2)}, u32[]{:S(2)}) async-start(f32[16,8,256]{2,1,0:T(8,128)} %shard_map.172), calls=%async_computation.1 | async-start | bytes 262144 | tf_op jit(solution)/shard_map/all_to_all | solution.py:521
  31.3 42.7 %copy-start = (bf16[64,8,8,128]{3,2,1,0:T(8,128)(2,1)S(1)}, bf16[64,8,8,128]{3,2,1,0:T(8,128)(2,1)}, u32[]{:S(2)}) copy-start(bf16[64,8,8,128]{3,2,1,0:T(8,128)(2,1)} %flow.3) | copy-start | bytes 3145732
  31.3 42.7 %copy-start.1 = (bf16[256,256]{1,0:T(8,128)(2,1)S(1)}, bf16[256,256]{1,0:T(8,128)(2,1)}, u32[]{:S(2)}) copy-start(bf16[256,256]{1,0:T(8,128)(2,1)} %constant.8.clone.zf) | copy-start | bytes 393220
  104.2 2.4 %collective-permute-start = (f32[16,8,768]{2,1,0:T(8,128)S(1)}, f32[16,8,768]{2,1,0:T(8,128)S(1)}, u32[]{:S(2)}, u32[]{:S(2)}) collective-permute-start(f32[16,8,768]{2,1,0:T(8,128)S(1)} %all_to_all.34.data), channel_id=1, source_target_pairs={{0,1},{1,0},{2,3},{3,2},{4,5},{5,4},{6,7},{7,6},{8,9},{9,8},{10,11... | collective-permute-start | bytes 1179656 | tf_op jit(solution)/shard_map/ppermute | solution.py:583
